TPU v7x, 32 devices: a whole 2x2x4 slice. The times are simulated.
32 devices in a mesh: gz: 8 (over z, y), gy: 4 (over x, core).
Axes of the slice: x: 2, y: 2, z: 4, core: 2. Of those that a mesh axis runs over, the one named last changes fastest.
Arguments:
- charges: float32 [64, 64, 1024], P('gz', 'gy'), may hold values from -6 to 6
- kernel: float32 [64, 64, 64], P('gz', 'gy'), may hold values from -0.01171875 to 0.01171875
Outputs:
- fine_potential: float32 [128, 128, 2048], P('gz', 'gy')
All inputs are finite; a program needn't handle non-finite values.
Results may differ from a plain program's by a relative error of at most 0.000098.
Values sent between devices are 32-bit elements; how exact they have to be, the bound alone decides.
A program may use at most 128 MiB of HBM per device.

v0:
```python
import functools

import jax
import jax.numpy as jnp
import numpy as np
from jax import lax
from jax.experimental import pallas as pl
from jax.experimental.pallas import tpu as pltpu
from jax.sharding import PartitionSpec as P

AXES = ("gz", "gy")


def angle(first, second, count):
    return 2.0 * np.pi / count * ((first * second) % count)


def x_table(count, replicas, devices):
    half = replicas // 2
    columns = count * half // devices
    device, part, column, x, side, pair = np.ix_(
        *(np.arange(s) for s in (devices, 2, columns, count, 2, half))
    )
    flat = device * columns + column
    theta = angle(flat // half, x, count)
    value = np.where(part == side, np.cos(theta), np.where(part == 0, np.sin(theta), -np.sin(theta)))
    value = value * (flat % half == pair)
    return value.reshape(devices * 2 * columns, count, replicas)


def x_kernel_table(count, replicas, devices):
    half = replicas // 2
    columns = count * half // devices
    lines = max(1, columns // half)
    device, part, line, x = np.ix_(*(np.arange(s) for s in (devices, 2, lines, count)))
    theta = angle(device * columns // half + line, x, count)
    value = np.where(part == 0, np.cos(theta), -np.sin(theta))
    return value.reshape(devices * 2 * lines, count)


def y_table(count, planes, rows):
    part, block, plane, row, new_plane, new_part, freq = np.ix_(
        *(np.arange(s) for s in (2, count // rows, planes, rows, planes, 2, count))
    )
    theta = angle(block * rows + row, freq, count)
    value = np.where(
        part == new_part, np.cos(theta), np.where(new_part == 0, np.sin(theta), -np.sin(theta))
    )
    value = value * (plane == new_plane)
    return value.reshape(2 * count * planes, planes * 2 * count)


def z_table(count, planes, columns, lines, group, wave):
    blocks = count // planes
    low, high, column, z_low, z_high, line = np.ix_(
        *(np.arange(s) for s in (planes, blocks, columns, planes, blocks, lines))
    )
    theta = angle(high * planes + low, z_high * planes + z_low, count)
    value = wave(theta) * (column // group == line)
    return value.reshape(count * columns, count * lines)


def refined(values, axis):
    before = np.roll(values, 1, axis)
    after = np.roll(values, -1, axis)
    after_two = np.roll(values, -2, axis)
    middle = (9.0 * (values + after) - (before + after_two)) / 16.0
    stacked = np.stack([values, middle], axis=axis + 1)
    shape = list(values.shape)
    shape[axis] = 2 * shape[axis]
    return stacked.reshape(shape)


def const(values):
    return jnp.asarray(np.asarray(values, np.float32))


def dot(left, right, dims=((1,), (0,))):
    return lax.dot_general(
        left, right, (dims, ((), ())), precision=lax.Precision.HIGH,
        preferred_element_type=jnp.float32,
    )


def extended(block, axis, dim):
    size = lax.axis_size(axis)
    forward = [(i, (i + 1) % size) for i in range(size)]
    backward = [(target, source) for source, target in forward]
    low = lax.ppermute(lax.slice_in_dim(block, block.shape[dim] - 1, None, axis=dim), axis, forward)
    high = lax.ppermute(lax.slice_in_dim(block, 0, 2, axis=dim), axis, backward)
    return jnp.concatenate([low, block, high], axis=dim)


def refine_rim(haloed, axis, count):
    centre = lax.slice_in_dim(haloed, 1, 1 + count, axis=axis)
    before = lax.slice_in_dim(haloed, 0, count, axis=axis)
    after = lax.slice_in_dim(haloed, 2, 2 + count, axis=axis)
    after_two = lax.slice_in_dim(haloed, 3, 3 + count, axis=axis)
    middle = (9.0 * (centre + after) - (before + after_two)) / 16.0
    stacked = jnp.stack([centre, middle], axis=axis + 1)
    shape = list(centre.shape)
    shape[axis] = 2 * count
    return stacked.reshape(shape)


def plain(charges, kernel):
    planes, rows, count = kernel.shape
    replicas = charges.shape[2] // count
    half = replicas // 2
    blocks_z, blocks_y = lax.axis_size("gz"), lax.axis_size("gy")
    devices = blocks_z * blocks_y
    place = planes * rows
    columns = count * half // devices
    lines = max(1, columns // half)
    table_x = x_table(count, replicas, devices)
    table_y = const(y_table(count, planes, rows))
    cos_z = const(z_table(count, planes, columns, columns, 1, np.cos))
    sin_z = const(z_table(count, planes, columns, columns, 1, np.sin))
    cos_k = const(z_table(count, planes, columns, lines, half, np.cos) / count**3)
    sin_k = const(z_table(count, planes, columns, lines, half, np.sin) / count**3)

    sent = dot(const(table_x.reshape(-1, count * replicas)), charges.reshape(place, -1), ((1,), (1,)))
    sent_k = dot(const(x_kernel_table(count, replicas, devices)), kernel.reshape(place, count), ((1,), (1,)))
    both = jnp.concatenate(
        [sent.reshape(devices, 2 * columns, place), sent_k.reshape(devices, 2 * lines, place)], axis=1
    )
    both = lax.all_to_all(both, AXES, split_axis=0, concat_axis=0, tiled=True)

    def by_y(block, width):
        block = block.reshape(blocks_z, blocks_y, 2, width, place).transpose(0, 3, 2, 1, 4)
        block = dot(block.reshape(blocks_z * width, 2 * blocks_y * place), table_y)
        block = block.reshape(blocks_z * width, planes, 2 * count).transpose(1, 0, 2)
        return block.reshape(count * width, 2 * count)

    def swap(values):
        return jnp.concatenate([values[:, count:], values[:, :count]], axis=1)

    sign = jnp.where(lax.broadcasted_iota(jnp.int32, (1, 2 * count), 1) < count, 1.0, -1.0)
    data = by_y(both[:, : 2 * columns], columns)
    green = by_y(both[:, 2 * columns :], lines)
    data = dot(cos_z, data) + sign * swap(dot(sin_z, data))
    green = dot(cos_k, green) + sign * swap(dot(sin_k, green))
    real, imag = green[:, :count], green[:, count:]
    data = data * jnp.concatenate([real, real], axis=1) + swap(data) * jnp.concatenate([-imag, imag], axis=1)
    data = dot(cos_z, data) - sign * swap(dot(sin_z, data))
    data = data.reshape(planes, blocks_z * columns, 2 * count).transpose(1, 0, 2)
    data = dot(data.reshape(blocks_z * columns, planes * 2 * count), table_y, ((1,), (1,)))
    data = data.reshape(blocks_z, columns, 2, blocks_y, place).transpose(0, 3, 2, 1, 4)
    data = lax.all_to_all(
        data.reshape(devices, 2 * columns, place), AXES, split_axis=0, concat_axis=0, tiled=True
    )
    fine_x = const(refined(table_x, 1).reshape(-1, 2 * count * replicas))
    result = dot(data.reshape(devices * 2 * columns, place), fine_x, ((0,), (0,)))
    result = result.reshape(planes, rows, 2 * count * replicas)
    result = extended(extended(result, "gz", 0), "gy", 1)
    result = refine_rim(result, 0, planes)
    return refine_rim(result, 1, rows)


LANES = 128
MESH = pl.DeviceIdType.MESH


def table(values):
    high = np.asarray(values, np.float32).astype(jnp.bfloat16)
    low = (np.asarray(values, np.float64) - high.astype(np.float64)).astype(jnp.bfloat16)
    return [jnp.asarray(high), jnp.asarray(low)]


def split(values):
    high = values.astype(jnp.bfloat16)
    return high, (values - high.astype(jnp.float32)).astype(jnp.bfloat16)


def mul(left, right, dims=((1,), (0,))):
    return lax.dot_general(left, right, (dims, ((), ())), preferred_element_type=jnp.float32)


def mul3(left, right, dims=((1,), (0,))):
    (a, b), (c, d) = left, right
    return mul(a, d, dims) + mul(b, c, dims) + mul(a, c, dims)


GROUPS = 4
ORDER = (2, 3, 1, 0)


def send_group(blocks_z, blocks_y, offset, x_ref, o_ref, sems, own_sem):
    size = blocks_z * blocks_y // GROUPS
    me = lax.axis_index("gz") * blocks_y + lax.axis_index("gy")
    target = lax.rem(me // size + offset, GROUPS)
    copies = []
    for step in range(size):
        if offset == 0 and step == 0:
            copy = pltpu.make_async_copy(x_ref.at[me], o_ref.at[me], own_sem)
        else:
            other = target * size + lax.rem(lax.rem(me, size) + step, size)
            number = offset * size + step
            copy = pltpu.make_async_remote_copy(
                src_ref=x_ref.at[other], dst_ref=o_ref.at[me],
                send_sem=sems[0].at[number], recv_sem=sems[1].at[number],
                device_id=(other // blocks_y, lax.rem(other, blocks_y)), device_id_type=MESH,
            )
        copy.start()
        copies.append(copy)
    return copies


def remote(source, target, sems, number, place):
    copy = pltpu.make_async_remote_copy(
        src_ref=source, dst_ref=target, send_sem=sems.at[0, number], recv_sem=sems.at[1, number],
        device_id=place, device_id_type=MESH,
    )
    copy.start()
    return copy


def main_kernel(sizes, *refs):
    columns, count, blocks_z, blocks_y, n_tables = sizes
    devices = blocks_z * blocks_y
    q_ref, k_ref = refs[0], refs[1]
    sources = refs[2 : 2 + n_tables]
    out = refs[2 + n_tables]
    tables = refs[3 + n_tables : 3 + 2 * n_tables]
    (sent, held, back, home, coarse, up, down, from_low, from_high,
     table_sem, send_a, recv_a, send_b, recv_b, own_sem, halo_sem) = refs[3 + 2 * n_tables :]
    loads = [pltpu.make_async_copy(s, t, table_sem.at[i]) for i, (s, t) in enumerate(zip(sources, tables))]
    for load in loads:
        load.start()
    gz, gy = lax.axis_index("gz"), lax.axis_index("gy")
    me = gz * blocks_y + gy
    barrier = pltpu.get_barrier_semaphore()
    for step in range(1, devices):
        other = lax.rem(me + step, devices)
        pl.semaphore_signal(
            barrier, inc=1, device_id=(other // blocks_y, lax.rem(other, blocks_y)), device_id_type=MESH
        )
    for load in loads[:4]:
        load.wait()
    width = q_ref.shape[1]
    size = devices // GROUPS
    deep = size * 2 * columns
    green = mul3((tables[2][...], tables[3][...]), split(k_ref[...]), ((1,), (1,)))
    sent[:, 2 * columns :, :] = green.reshape(devices, 8, LANES)
    charges = split(q_ref[...])

    def table_rows(group):
        place = pl.ds(pl.multiple_of(group * deep, deep), deep)
        return tables[0][place, :], tables[1][place, :]

    copies = []
    for offset in ORDER:
        group = lax.rem(me // size + offset, GROUPS)
        made = mul3(table_rows(group), charges, ((1,), (1,)))
        sent[pl.ds(group * size, size), : 2 * columns, :] = made.reshape(size, 2 * columns, LANES)
        if not copies:
            pl.semaphore_wait(barrier, devices - 1)
        copies += send_group(blocks_z, blocks_y, offset, sent, held, (send_a, recv_a), own_sem.at[0])
    for load in loads[4:]:
        load.wait()
    for copy in copies:
        copy.wait()
    pairs = [(tables[i][...], tables[i + 1][...]) for i in range(4, n_tables, 2)]
    middle_stage(columns, count, blocks_z, blocks_y, held, pairs, back)
    copies = [
        send_group(blocks_z, blocks_y, offset, back, home, (send_b, recv_b), own_sem.at[1])
        for offset in ORDER
    ]
    planes, rows, _ = coarse.shape
    made = jnp.zeros((LANES, width), jnp.float32)
    for offset, group_copies in zip(ORDER, copies):
        for copy in group_copies:
            copy.wait()
        group = lax.rem(me // size + GROUPS - offset, GROUPS)
        turned = jnp.transpose(home[pl.ds(group * size, size)].reshape(deep, LANES))
        made += mul3(split(turned), table_rows(group))
    made = made.reshape(planes, rows, width)
    coarse[...] = made
    above = (lax.rem(gz + 1, blocks_z), gy)
    below = (lax.rem(gz + blocks_z - 1, blocks_z), gy)
    copies = [
        remote(coarse.at[pl.ds(planes - 1, 1)], out.at[pl.ds(0, 1), pl.ds(0, rows)], halo_sem, 0, above),
        remote(coarse.at[pl.ds(0, 2)], out.at[pl.ds(planes + 1, 2), pl.ds(0, rows)], halo_sem, 1, below),
    ]
    out[1 : planes + 1, :rows, :] = made
    for p in range(1, planes + 1):
        up[p : p + 1, :] = coarse[p - 1, rows - 1 : rows, :]
        down[2 * p : 2 * p + 2, :] = coarse[p - 1, 0:2, :]
    for copy in copies:
        copy.wait()
    for p in (0, planes + 1, planes + 2):
        up[p : p + 1, :] = out[p, rows - 1 : rows, :]
        down[2 * p : 2 * p + 2, :] = out[p, 0:2, :]
    above = (gz, lax.rem(gy + 1, blocks_y))
    below = (gz, lax.rem(gy + blocks_y - 1, blocks_y))
    copies = [remote(up, from_low, halo_sem, 2, above), remote(down, from_high, halo_sem, 3, below)]
    for copy in copies:
        copy.wait()
    empty = jnp.zeros((5, width), jnp.float32)
    for p in range(planes + 3):
        rim = [from_low[p : p + 1, :], from_high[2 * p : 2 * p + 2, :], empty]
        out[p, rows : rows + 8, :] = jnp.concatenate(rim, axis=0)


def middle_stage(columns, count, blocks_z, blocks_y, held, tables, o_ref):
    planes = count // blocks_z
    table_y, cos_z, sin_z, green_a, green_b = tables
    x_ref = held[...].reshape(blocks_z, blocks_y, *held.shape[1:])
    lane = lax.broadcasted_iota(jnp.int32, (1, LANES), 1)
    sign = jnp.where(lane < count, 1.0, -1.0)

    def swap(values):
        return pltpu.roll(values, count, 1)

    def lines_first(values):
        return jnp.concatenate([values[:, p * LANES : (p + 1) * LANES] for p in range(planes)], axis=0)

    data = jnp.concatenate(
        [
            x_ref[:, y, c * columns : (c + 1) * columns, :].reshape(blocks_z * columns, LANES)
            for c in range(2)
            for y in range(blocks_y)
        ],
        axis=1,
    )
    green = jnp.concatenate(
        [x_ref[:, y, 2 * columns :, :].reshape(blocks_z * 8, LANES) for y in range(blocks_y)], axis=1
    )
    data = lines_first(mul3(split(data), table_y))
    deep = blocks_y * LANES
    green = lines_first(mul3(split(green), tuple(t[:deep, :] for t in table_y)))
    green = split(green)
    green = mul3(green_a, green) - sign * swap(mul3(green_b, green))
    half = cos_z[0].shape[0] // count

    def parts(values):
        values = values.reshape(count, columns, LANES)
        return [
            values[:, m : m + half, :].reshape(count * half, LANES) for m in range(0, columns, half)
        ]

    made = []
    for part, factor in zip(parts(data), parts(green)):
        part = split(part)
        part = mul3(cos_z, part) + sign * swap(mul3(sin_z, part))
        other = swap(factor)
        real = jnp.where(lane < count, factor, other)
        imag = jnp.where(lane < count, -other, factor)
        part = split(part * real + swap(part) * imag)
        part = mul3(cos_z, part) - sign * swap(mul3(sin_z, part))
        made.append(part.reshape(count, half, LANES))
    data = jnp.concatenate(made, axis=1).reshape(count * columns, LANES)
    size = blocks_z * columns
    data = jnp.concatenate([data[p * size : (p + 1) * size, :] for p in range(planes)], axis=1)
    data = mul3(split(data), table_y, ((1,), (1,)))
    for c in range(2):
        pieces = [
            data[:, (c * blocks_y + y) * LANES : (c * blocks_y + y + 1) * LANES].reshape(
                blocks_z, 1, columns, LANES
            )
            for y in range(blocks_y)
        ]
        piece = jnp.concatenate(pieces, axis=1).reshape(blocks_z * blocks_y, columns, LANES)
        o_ref[:, c * columns : (c + 1) * columns, :] = piece


def refine_kernel(x_ref, r_ref, t_ref, o_ref):
    step = pl.program_id(0)
    near = x_ref[pl.ds(step, 4)].reshape(4 * x_ref.shape[1], x_ref.shape[2])
    high, low = split(near)
    fine = mul(r_ref[...], low) + mul(r_ref[...], high)
    high, low = split(fine)
    blocks = fine.shape[1] // LANES
    def windows(values):
        made = []
        for b in range(blocks):
            pieces = [(b + s) % blocks * LANES for s in (-1, 0, 1)]
            made.append(jnp.concatenate([values[:, p : p + LANES] for p in pieces], axis=1))
        return jnp.concatenate(made, axis=0)

    made = mul(windows(low), t_ref[...]) + mul(windows(high), t_ref[...])
    for b in range(blocks):
        piece = made[b * fine.shape[0] : (b + 1) * fine.shape[0], :]
        o_ref[:, :, 2 * b * LANES : 2 * (b + 1) * LANES] = piece.reshape(2, -1, 2 * LANES)


def rim_table(count):
    made = np.zeros((2 * count, count + 3))
    for i in range(count):
        made[2 * i, i + 1] = 1.0
        made[2 * i + 1, i : i + 4] = np.array([-1.0, 9.0, 9.0, -1.0]) / 16.0
    return made


def refine(haloed, planes, rows, width, replicas):
    along_y = rim_table(rows)
    empty = np.zeros((2 * rows, 5))
    along_y = np.concatenate([along_y[:, 1 : rows + 1], along_y[:, :1], along_y[:, rows + 1 :], empty], axis=1)
    both = jnp.asarray(np.kron(rim_table(1), along_y), jnp.bfloat16)
    count = width // replicas
    spread = refined(np.eye(width).reshape(width, count, replicas), 1).reshape(width, 2 * width)
    spread = jnp.asarray(spread[: 3 * LANES, 2 * LANES : 4 * LANES], jnp.bfloat16)
    return pl.pallas_call(
        refine_kernel,
        grid=(planes,),
        out_shape=jax.ShapeDtypeStruct((2 * planes, 2 * rows, 2 * width), jnp.float32),
        in_specs=[
            pl.BlockSpec(haloed.shape, lambda i: (0, 0, 0)),
            pl.BlockSpec(both.shape, lambda i: (0, 0)),
            pl.BlockSpec(spread.shape, lambda i: (0, 0)),
        ],
        out_specs=pl.BlockSpec((2, 2 * rows, 2 * width), lambda i: (i, 0, 0)),
    )(haloed, both, spread)


def z_green_table(count, planes, columns, group, first, second):
    lines = max(1, columns // group)
    rows = []
    for wave in (first, second):
        made = z_table(count, planes, columns, lines, group, wave)
        rows.append(made.reshape(count * columns, count, lines))
    made = np.concatenate(rows, axis=2)
    made = np.pad(made, ((0, 0), (0, 0), (0, 8 - 2 * lines)))
    return made.reshape(count * columns, count * 8)


def per_device(charges, kernel):
    planes, rows, count = kernel.shape
    width = charges.shape[2]
    replicas = width // count
    half = replicas // 2
    blocks_z, blocks_y = lax.axis_size("gz"), lax.axis_size("gy")
    devices = blocks_z * blocks_y
    place = planes * rows
    columns = count * half // devices
    lines = max(1, columns // half)
    fits = place == LANES and 2 * count == LANES and columns % 8 == 0 and 2 * lines <= 8
    if not fits or LANES % replicas or width < 3 * LANES or rows % 8 or planes < 2 \
            or devices % GROUPS or half % 8 or columns % half:
        return plain(charges, kernel)
    table_x = table(x_table(count, replicas, devices).reshape(-1, width))
    lines_x = x_kernel_table(count, replicas, devices).reshape(devices, 2 * lines, count)
    lines_x = table(np.pad(lines_x, ((0, 0), (0, 8 - 2 * lines), (0, 0))).reshape(devices * 8, count))
    table_y = table(y_table(count, planes, rows))
    cos_z = table(z_table(count, planes, half, half, 1, np.cos))
    sin_z = table(z_table(count, planes, half, half, 1, np.sin))
    scale = 1.0 / count**3
    green_a = table(scale * z_green_table(count, planes, columns, half, np.cos, np.sin))
    green_b = table(scale * z_green_table(count, planes, columns, half, lambda t: -np.sin(t), np.cos))

    tables = [*table_x, *lines_x, *table_y, *cos_z, *sin_z, *green_a, *green_b]
    size = 2 * columns
    packed = -(-(planes + 3) // 8) * 8
    vmem = pl.BlockSpec(memory_space=pltpu.VMEM)
    block = lambda *shape: pltpu.VMEM(shape, jnp.float32)
    haloed = pl.pallas_call(
        functools.partial(main_kernel, (columns, count, blocks_z, blocks_y, len(tables))),
        out_shape=jax.ShapeDtypeStruct((planes + 3, rows + 8, width), jnp.float32),
        in_specs=[vmem, vmem] + [pl.BlockSpec(memory_space=pl.ANY)] * len(tables),
        out_specs=vmem,
        scratch_shapes=[
            *(pltpu.VMEM(t.shape, t.dtype) for t in tables),
            block(devices, size + 8, LANES), block(devices, size + 8, LANES),
            block(devices, size, LANES), block(devices, size, LANES),
            block(planes, rows, width),
            block(packed, width), block(2 * packed, width),
            block(packed, width), block(2 * packed, width),
            pltpu.SemaphoreType.DMA((len(tables),)),
            *(pltpu.SemaphoreType.DMA((devices,)) for _ in range(4)),
            pltpu.SemaphoreType.DMA((2,)),
            pltpu.SemaphoreType.DMA((2, 4)),
        ],
        compiler_params=pltpu.CompilerParams(
            collective_id=0, has_side_effects=True, vmem_limit_bytes=60 * 1024 * 1024
        ),
    )(charges.reshape(place, width), kernel.reshape(place, count), *tables)
    return refine(haloed, planes, rows, width, replicas)


def solution(mesh):
    placed = (P("gz", "gy", None), P("gz", "gy", None))
    return jax.shard_map(
        per_device, mesh=mesh, in_specs=placed, out_specs=P("gz", "gy", None), check_vma=False
    )
```

profile of v0, /device:TPU:0, one launch (start us, length us, event | category | flops | bytes accessed | tf_op | source)
XLA Modules:
  0.0 65.2 jit_solution(16117222451116883876)
XLA Ops:
  0.0 57.7 %shard_map.172.x_ref = f32[11,24,1024]{2,1,0:T(8,128)} custom-call(f32[128,1024]{1,0:T(8,128)} %bitcast.2, f32[128,64]{1,0:T(8,128)} %bitcast.3, bf16[1024,1024]{1,0:T(8,128)(2,1)} %constant.32.clone.refs_2_, bf16[1024,1024]{1,0:T(8,128)(2,1)} %constant.33.clone.refs_3_, bf16[256,64]{1,0:T(8,128)(2,1)} %constant.34.clone.refs_4_, ...), custom_call_target="tpu_custom_call" | custom-call | tf_op jit(solution)/shard_map/pallas_call | solution.py:456
  57.7 7.5 %shard_map.173 = f32[16,32,2048]{2,1,0:T(8,128)} custom-call(f32[11,24,1024]{2,1,0:T(8,128)} %shard_map.172.x_ref, bf16[64,96]{1,0:T(8,128)(2,1)} %constant.46.clone.r_ref, bf16[384,256]{1,0:T(8,128)(2,1)} %constant.47.clone.t_ref), custom_call_target="tpu_custom_call" | custom-call | tf_op jit(solution)/shard_map/pallas_call | solution.py:403
where the time goes:
time: 65.8 us; the launch traced here: 65.2 us
  Pallas kernels  65.2 us (99%)
    pallas_call x1, Pallas kernels, per_device(): pl.pallas_call(functools.partial(main_kernel, (columns, count, blocks_z,...  57.7 us
    pallas_call x1, Pallas kernels, refine(): pl.pallas_call(refine_kernel, grid=(planes,), out_shape=jax.ShapeDtypeStr...  7.47 us

commit v1 on v0

v1 whole, which is shorter than its diff:
```python
import functools

import jax
import jax.numpy as jnp
import numpy as np
from jax import lax
from jax.experimental import pallas as pl
from jax.experimental.pallas import tpu as pltpu
from jax.sharding import PartitionSpec as P

AXES = ("gz", "gy")


def angle(first, second, count):
    return 2.0 * np.pi / count * ((first * second) % count)


def x_table(count, replicas, devices):
    half = replicas // 2
    columns = count * half // devices
    device, part, column, x, side, pair = np.ix_(
        *(np.arange(s) for s in (devices, 2, columns, count, 2, half))
    )
    flat = device * columns + column
    theta = angle(flat // half, x, count)
    value = np.where(part == side, np.cos(theta), np.where(part == 0, np.sin(theta), -np.sin(theta)))
    value = value * (flat % half == pair)
    return value.reshape(devices * 2 * columns, count, replicas)


def x_kernel_table(count, replicas, devices):
    half = replicas // 2
    columns = count * half // devices
    lines = max(1, columns // half)
    device, part, line, x = np.ix_(*(np.arange(s) for s in (devices, 2, lines, count)))
    theta = angle(device * columns // half + line, x, count)
    value = np.where(part == 0, np.cos(theta), -np.sin(theta))
    return value.reshape(devices * 2 * lines, count)


def y_table(count, planes, rows):
    part, block, plane, row, new_plane, new_part, freq = np.ix_(
        *(np.arange(s) for s in (2, count // rows, planes, rows, planes, 2, count))
    )
    theta = angle(block * rows + row, freq, count)
    value = np.where(
        part == new_part, np.cos(theta), np.where(new_part == 0, np.sin(theta), -np.sin(theta))
    )
    value = value * (plane == new_plane)
    return value.reshape(2 * count * planes, planes * 2 * count)


def z_table(count, planes, columns, lines, group, wave):
    blocks = count // planes
    low, high, column, z_low, z_high, line = np.ix_(
        *(np.arange(s) for s in (planes, blocks, columns, planes, blocks, lines))
    )
    theta = angle(high * planes + low, z_high * planes + z_low, count)
    value = wave(theta) * (column // group == line)
    return value.reshape(count * columns, count * lines)


def refined(values, axis):
    before = np.roll(values, 1, axis)
    after = np.roll(values, -1, axis)
    after_two = np.roll(values, -2, axis)
    middle = (9.0 * (values + after) - (before + after_two)) / 16.0
    stacked = np.stack([values, middle], axis=axis + 1)
    shape = list(values.shape)
    shape[axis] = 2 * shape[axis]
    return stacked.reshape(shape)


def const(values):
    return jnp.asarray(np.asarray(values, np.float32))


def dot(left, right, dims=((1,), (0,))):
    return lax.dot_general(
        left, right, (dims, ((), ())), precision=lax.Precision.HIGH,
        preferred_element_type=jnp.float32,
    )


def extended(block, axis, dim):
    size = lax.axis_size(axis)
    forward = [(i, (i + 1) % size) for i in range(size)]
    backward = [(target, source) for source, target in forward]
    low = lax.ppermute(lax.slice_in_dim(block, block.shape[dim] - 1, None, axis=dim), axis, forward)
    high = lax.ppermute(lax.slice_in_dim(block, 0, 2, axis=dim), axis, backward)
    return jnp.concatenate([low, block, high], axis=dim)


def refine_rim(haloed, axis, count):
    centre = lax.slice_in_dim(haloed, 1, 1 + count, axis=axis)
    before = lax.slice_in_dim(haloed, 0, count, axis=axis)
    after = lax.slice_in_dim(haloed, 2, 2 + count, axis=axis)
    after_two = lax.slice_in_dim(haloed, 3, 3 + count, axis=axis)
    middle = (9.0 * (centre + after) - (before + after_two)) / 16.0
    stacked = jnp.stack([centre, middle], axis=axis + 1)
    shape = list(centre.shape)
    shape[axis] = 2 * count
    return stacked.reshape(shape)


def plain(charges, kernel):
    planes, rows, count = kernel.shape
    replicas = charges.shape[2] // count
    half = replicas // 2
    blocks_z, blocks_y = lax.axis_size("gz"), lax.axis_size("gy")
    devices = blocks_z * blocks_y
    place = planes * rows
    columns = count * half // devices
    lines = max(1, columns // half)
    table_x = x_table(count, replicas, devices)
    table_y = const(y_table(count, planes, rows))
    cos_z = const(z_table(count, planes, columns, columns, 1, np.cos))
    sin_z = const(z_table(count, planes, columns, columns, 1, np.sin))
    cos_k = const(z_table(count, planes, columns, lines, half, np.cos) / count**3)
    sin_k = const(z_table(count, planes, columns, lines, half, np.sin) / count**3)

    sent = dot(const(table_x.reshape(-1, count * replicas)), charges.reshape(place, -1), ((1,), (1,)))
    sent_k = dot(const(x_kernel_table(count, replicas, devices)), kernel.reshape(place, count), ((1,), (1,)))
    both = jnp.concatenate(
        [sent.reshape(devices, 2 * columns, place), sent_k.reshape(devices, 2 * lines, place)], axis=1
    )
    both = lax.all_to_all(both, AXES, split_axis=0, concat_axis=0, tiled=True)

    def by_y(block, width):
        block = block.reshape(blocks_z, blocks_y, 2, width, place).transpose(0, 3, 2, 1, 4)
        block = dot(block.reshape(blocks_z * width, 2 * blocks_y * place), table_y)
        block = block.reshape(blocks_z * width, planes, 2 * count).transpose(1, 0, 2)
        return block.reshape(count * width, 2 * count)

    def swap(values):
        return jnp.concatenate([values[:, count:], values[:, :count]], axis=1)

    sign = jnp.where(lax.broadcasted_iota(jnp.int32, (1, 2 * count), 1) < count, 1.0, -1.0)
    data = by_y(both[:, : 2 * columns], columns)
    green = by_y(both[:, 2 * columns :], lines)
    data = dot(cos_z, data) + sign * swap(dot(sin_z, data))
    green = dot(cos_k, green) + sign * swap(dot(sin_k, green))
    real, imag = green[:, :count], green[:, count:]
    data = data * jnp.concatenate([real, real], axis=1) + swap(data) * jnp.concatenate([-imag, imag], axis=1)
    data = dot(cos_z, data) - sign * swap(dot(sin_z, data))
    data = data.reshape(planes, blocks_z * columns, 2 * count).transpose(1, 0, 2)
    data = dot(data.reshape(blocks_z * columns, planes * 2 * count), table_y, ((1,), (1,)))
    data = data.reshape(blocks_z, columns, 2, blocks_y, place).transpose(0, 3, 2, 1, 4)
    data = lax.all_to_all(
        data.reshape(devices, 2 * columns, place), AXES, split_axis=0, concat_axis=0, tiled=True
    )
    fine_x = const(refined(table_x, 1).reshape(-1, 2 * count * replicas))
    result = dot(data.reshape(devices * 2 * columns, place), fine_x, ((0,), (0,)))
    result = result.reshape(planes, rows, 2 * count * replicas)
    result = extended(extended(result, "gz", 0), "gy", 1)
    result = refine_rim(result, 0, planes)
    return refine_rim(result, 1, rows)


LANES = 128
MESH = pl.DeviceIdType.MESH


def table(values):
    high = np.asarray(values, np.float32).astype(jnp.bfloat16)
    low = (np.asarray(values, np.float64) - high.astype(np.float64)).astype(jnp.bfloat16)
    return [jnp.asarray(high), jnp.asarray(low)]


def split(values):
    high = values.astype(jnp.bfloat16)
    return high, (values - high.astype(jnp.float32)).astype(jnp.bfloat16)


def mul(left, right, dims=((1,), (0,))):
    return lax.dot_general(left, right, (dims, ((), ())), preferred_element_type=jnp.float32)


def mul3(left, right, dims=((1,), (0,))):
    (a, b), (c, d) = left, right
    return mul(a, d, dims) + mul(b, c, dims) + mul(a, c, dims)


GROUPS = 4
CHUNKS = 2


def line_of(device, chunk, count):
    flip = np.where(device == 0, count // 2, (count - device) % count)
    return np.where(chunk == 0, device, flip)


def pair_table(count, replicas, devices):
    half = replicas // 2
    chunk, device, part, row, x, side, pair = np.ix_(
        *(np.arange(s) for s in (CHUNKS, devices, 2, half, count, 2, half))
    )
    theta = angle(line_of(device, chunk, count), x, count)
    value = np.where(part == side, np.cos(theta), np.where(part == 0, np.sin(theta), -np.sin(theta)))
    value = value * (row == pair)
    return value.reshape(CHUNKS, devices * 2 * half, count, replicas)


def line_table(count, devices):
    device, row, x = np.ix_(*(np.arange(s) for s in (devices, 8, count)))
    theta = angle(device, x, count)
    other = np.where(device == 0, np.cos(angle(count // 2, x, count)), -np.sin(theta))
    value = np.where(row == 0, np.cos(theta), np.where(row == 1, other, 0.0))
    return value.reshape(devices * 8, count)


def stack3(values):
    high = np.asarray(values, np.float32).astype(jnp.bfloat16)
    low = (np.asarray(values, np.float64) - high.astype(np.float64)).astype(jnp.bfloat16)
    return jnp.asarray(np.concatenate([high, high, low], axis=1))


def z_tables(count, blocks):
    planes = count // blocks
    freq = np.arange(count)[:, None]
    place = np.arange(count)[None, :]
    theta = angle(freq, (place % blocks) * planes + place // blocks, count)
    forward = stack3(np.concatenate([np.cos(theta), np.sin(theta)], axis=0))
    inverse = stack3(np.concatenate([np.cos(theta.T), np.sin(theta.T)], axis=0))
    return forward, inverse


def remote(source, target, sems, number, place):
    copy = pltpu.make_async_remote_copy(
        src_ref=source, dst_ref=target, send_sem=sems.at[0, number], recv_sem=sems.at[1, number],
        device_id=place, device_id_type=MESH,
    )
    copy.start()
    return copy


def exchange(blocks_z, blocks_y, rows, source, target, sems):
    size = blocks_z * blocks_y // GROUPS
    me = lax.axis_index("gz") * blocks_y + lax.axis_index("gy")
    group, inner = me // size, lax.rem(me, size)
    high, low = group // 2, lax.rem(group, 2)
    pitch_from, pitch_to = source.shape[0] // (size * GROUPS), target.shape[0] // (size * GROUPS)

    def span(ref, device, pitch):
        return ref.at[pl.ds(pl.multiple_of(device * pitch, 8), rows)]

    copies = []
    for flip_high, flip_low in ((1, 0), (1, 1), (0, 1), (0, 0)):
        other_group = lax.rem(high + flip_high, 2) * 2 + lax.rem(low + flip_low, 2)
        for step in range(size):
            if (flip_high, flip_low, step) == (0, 0, 0):
                continue
            other = other_group * size + lax.rem(inner + step, size)
            copies.append(remote(
                span(source, other, pitch_from), span(target, me, pitch_to), sems, len(copies),
                (other // blocks_y, lax.rem(other, blocks_y)),
            ))
    mine_from = pl.ds(pl.multiple_of(me * pitch_from, 8), min(pitch_from, pitch_to))
    mine_to = pl.ds(pl.multiple_of(me * pitch_to, 8), min(pitch_from, pitch_to))
    target[mine_to, :] = source[mine_from, :]
    return copies


def wait_recv(copies):
    for copy in copies:
        copy.wait_recv()


def swap_parts(values):
    half = LANES // 2
    pieces = [
        pltpu.roll(values[:, p : p + LANES], half, 1) for p in range(0, values.shape[1], LANES)
    ]
    return jnp.concatenate(pieces, axis=1)


def stacked(values):
    high, low = split(values)
    return jnp.concatenate([low, high, high], axis=0)


def repeat(values, times):
    return jnp.concatenate([values] * times, axis=1)


def y_lines(ref, start, stride, blocks):
    return ref[pl.ds(start, blocks, stride=stride), :]


def middle_stage(sizes, held, table_y, forward, inverse, green, back):
    count, blocks_z, blocks_y, half = sizes
    planes = count // blocks_z
    pitch = held.shape[0] // (blocks_z * blocks_y)
    lane = lax.broadcasted_iota(jnp.int32, (1, LANES), 1)
    sign = jnp.where(lane < count, 1.0, -1.0)

    def gather(row):
        pieces = [y_lines(held, y * pitch + row, blocks_y * pitch, blocks_z) for y in range(blocks_y)]
        return jnp.concatenate(pieces, axis=1)

    lines = [
        jnp.concatenate([gather(column), gather(half + column)], axis=1) for column in range(half)
    ]
    if green is None:
        me = lax.axis_index("gz") * blocks_y + lax.axis_index("gy")
        keep = jnp.where(me == 0, 0.0, 1.0).astype(jnp.float32)
        first, second = gather(2 * half), gather(2 * half + 1)
        lines.append(jnp.concatenate([first, keep * second], axis=1))
        lines.append(
            jnp.concatenate([keep * first + (1.0 - keep) * second, -keep * second], axis=1)
        )
    width = len(lines)
    data = mul3(split(jnp.concatenate(lines, axis=0)), table_y)
    data = jnp.concatenate(
        [
            jnp.concatenate(
                [
                    data[c * blocks_z : (c + 1) * blocks_z, p * LANES : (p + 1) * LANES]
                    for p in range(planes)
                ],
                axis=0,
            )
            for c in range(width)
        ],
        axis=1,
    )
    both = mul(forward, stacked(data))
    data = both[:count] + repeat(sign, width) * swap_parts(both[count:])
    spectra = None
    if green is None:
        scaled = data[:, half * LANES :] * (1.0 / count**3)
        green, spectra = scaled[:, :LANES], scaled
        data = data[:, : half * LANES]
    other = swap_parts(green)
    real = jnp.where(lane < count, green, other)
    imag = jnp.where(lane < count, -other, green)
    data = data * repeat(real, half) + swap_parts(data) * repeat(imag, half)
    both = mul(inverse, stacked(data))
    data = both[:count] - repeat(sign, half) * swap_parts(both[count:])
    data = jnp.concatenate(
        [
            jnp.concatenate(
                [
                    data[p * blocks_z : (p + 1) * blocks_z, c * LANES : (c + 1) * LANES]
                    for p in range(planes)
                ],
                axis=1,
            )
            for c in range(half)
        ],
        axis=0,
    )
    data = mul3(split(data), table_y, ((1,), (1,)))
    out_pitch = 2 * half
    for column in range(half):
        for part in range(2):
            for y in range(blocks_y):
                at = (part * blocks_y + y) * LANES
                back[pl.ds(y * out_pitch + part * half + column, blocks_z, stride=blocks_y * out_pitch), :] = (
                    data[column * blocks_z : (column + 1) * blocks_z, at : at + LANES]
                )
    return spectra


def send_rims(blocks_z, blocks_y, planes, rows, own, stage, rims, sems):
    to_up, to_down, to_corner = stage
    low_z, high_z, low_y, high_y, corner = rims
    gz, gy = lax.axis_index("gz"), lax.axis_index("gy")
    next_z, last_z = lax.rem(gz + 1, blocks_z), lax.rem(gz + blocks_z - 1, blocks_z)
    next_y, last_y = lax.rem(gy + 1, blocks_y), lax.rem(gy + blocks_y - 1, blocks_y)
    end = (planes - 1) * rows
    copies = [
        remote(own.at[pl.ds(0, 2 * rows)], high_z, sems, 0, (last_z, gy)),
        remote(own.at[pl.ds(end, rows)], low_z, sems, 1, (next_z, gy)),
    ]
    def side(row):
        return jnp.concatenate([own[p * rows + row : p * rows + row + 1, :] for p in range(planes)], axis=0)

    to_up[...] = side(rows - 1)
    to_down[...] = jnp.concatenate([side(0), side(1)], axis=0)
    picks = (
        (end + rows - 1,), (end, end + 1), (rows - 1, 2 * rows - 1), (0, 1, rows, rows + 1),
    )
    for number, pick in enumerate(picks):
        pieces = [own[r : r + 1, :] for r in pick]
        pieces.append(jnp.zeros((8 - len(pick), own.shape[1]), jnp.float32))
        to_corner[number] = jnp.concatenate(pieces, axis=0)
    copies.append(remote(to_down, high_y, sems, 2, (gz, last_y)))
    copies.append(remote(to_up, low_y, sems, 3, (gz, next_y)))
    places = ((next_z, next_y), (next_z, last_y), (last_z, next_y), (last_z, last_y))
    for number, (pick, place) in enumerate(zip(picks, places)):
        span = pl.ds(0, len(pick))
        copies.append(
            remote(to_corner.at[number, span], corner.at[number, span], sems, 4 + number, place)
        )
    return copies


def rim_lines(planes, rims):
    low_z, high_z, low_y, high_y, corner = rims
    empty = jnp.zeros((5, low_z.shape[1]), jnp.float32)
    tiles = [corner[0, 0:1, :], corner[1, 0:2, :], empty]
    for p in range(planes):
        tiles += [
            low_y[p : p + 1, :], high_y[p : p + 1, :], high_y[planes + p : planes + p + 1, :], empty,
        ]
    tiles += [corner[2, 0:1, :], corner[3, 0:2, :], empty]
    tiles += [corner[2, 1:2, :], corner[3, 2:4, :], empty]
    return jnp.concatenate([low_z[...], high_z[...], *tiles], axis=0)


def main_kernel(sizes, *refs):
    count, blocks_z, blocks_y, half, n_tables = sizes
    devices = blocks_z * blocks_y
    planes = count // blocks_z
    q_ref, k_ref = refs[:2]
    sources = refs[2 : 2 + n_tables]
    out = refs[2 + n_tables]
    tables = refs[3 + n_tables : 3 + 2 * n_tables]
    rest = list(refs[3 + 2 * n_tables :])
    table_sem, sent_sem, back_sem, rim_sem = rest[:4]
    sent, held, back, home, own = (rest[4 + 2 * i : 6 + 2 * i] for i in range(5))
    stages, rims = (rest[14:17], rest[17:20]), (rest[20:25], rest[25:30])
    table_x, table_k, table_y, table_z, table_f = (
        tables[0:2], tables[2:4], tables[4:6], tables[6:8], tables[8:12]
    )
    loads = [pltpu.make_async_copy(s, t, table_sem.at[i]) for i, (s, t) in enumerate(zip(sources, tables))]
    for load in loads:
        load.start()
    me = lax.axis_index("gz") * blocks_y + lax.axis_index("gy")
    barrier = pltpu.get_barrier_semaphore()
    for step in range(1, devices):
        other = lax.rem(me + step, devices)
        pl.semaphore_signal(
            barrier, inc=1, device_id=(other // blocks_y, lax.rem(other, blocks_y)), device_id_type=MESH
        )
    rows = q_ref.shape[0] // planes
    size = 2 * half
    charges = jnp.concatenate(split(q_ref[...]), axis=0)
    pitch = sent[0].shape[0] // devices

    def x_lines(chunk):
        per = LANES // size
        for group in range(devices // per):
            both = mul(table_x[chunk][group * 2 * LANES : (group + 1) * 2 * LANES, :], charges, ((1,), (1,)))
            made = both[:LANES, :LANES] + both[:LANES, LANES:] + both[LANES:, :LANES]
            step = sent[chunk].shape[0] // devices
            for inner in range(per):
                at = (group * per + inner) * step
                sent[chunk][at : at + size, :] = made[inner * size : (inner + 1) * size, :]

    loads[2].wait()
    loads[3].wait()
    lines = mul3((table_k[0][...], table_k[1][...]), split(k_ref[...]), ((1,), (1,)))
    for device in range(devices):
        sent[0][device * pitch + size : device * pitch + size + 8, :] = lines[device * 8 : (device + 1) * 8, :]
    loads[0].wait()
    x_lines(0)
    pl.semaphore_wait(barrier, devices - 1)
    there = [exchange(blocks_z, blocks_y, size + 2, sent[0], held[0], sent_sem.at[0])]
    loads[1].wait()
    x_lines(1)
    there.append(exchange(blocks_z, blocks_y, size, sent[1], held[1], sent_sem.at[1]))
    for load in loads[4:8]:
        load.wait()
    y_pair = (table_y[0][...], table_y[1][...])
    shape = (count, blocks_z, blocks_y, half)
    wait_recv(there[0])
    green = middle_stage(shape, held[0], y_pair, table_z[0][...], table_z[1][...], None, back[0])
    returns = [exchange(blocks_z, blocks_y, size, back[0], home[0], back_sem.at[0])]
    wait_recv(there[1])
    middle_stage(shape, held[1], y_pair, table_z[0][...], table_z[1][...], green[:, LANES:], back[1])
    returns.append(exchange(blocks_z, blocks_y, size, back[1], home[1], back_sem.at[1]))
    for load in loads[8:]:
        load.wait()
    borders = []
    for chunk in range(CHUNKS):
        fine = (table_f[2 * chunk][...], table_f[2 * chunk + 1][...])
        wait_recv(returns[chunk])
        turned = jnp.transpose(home[chunk][...])
        own[chunk][...] = turned
        borders.append(
            send_rims(blocks_z, blocks_y, planes, rows, own[chunk], stages[chunk], rims[chunk], rim_sem.at[chunk])
        )
        made = mul3(split(turned), fine).reshape(planes, rows, -1)
        if chunk:
            made = out[1 : planes + 1, :rows, :] + made
        out[1 : planes + 1, :rows, :] = made
        wait_recv(borders[chunk])
        made = mul3(split(rim_lines(planes, rims[chunk])), fine)
        deep = 3 * rows
        ends, sides = made[:deep].reshape(3, rows, -1), made[deep:].reshape(planes + 3, 8, -1)
        if chunk:
            sides = out[:, rows:, :] + sides
            ends = jnp.concatenate([out[0:1, :rows, :], out[planes + 1 :, :rows, :]], axis=0) + ends
        out[:, rows:, :] = sides
        out[0:1, :rows, :] = ends[0:1]
        out[planes + 1 :, :rows, :] = ends[1:]
    for copies in there + returns + borders:
        for copy in copies:
            copy.wait_send()


def refine_kernel(x_ref, r_ref, o_ref):
    step = pl.program_id(0)
    near = x_ref[pl.ds(step, 4)].reshape(4 * x_ref.shape[1], x_ref.shape[2])
    high, low = split(near)
    fine = mul(r_ref[...], jnp.concatenate([low, high], axis=0))
    o_ref[...] = fine.reshape(o_ref.shape)


def rim_table(count):
    made = np.zeros((2 * count, count + 3))
    for i in range(count):
        made[2 * i, i + 1] = 1.0
        made[2 * i + 1, i : i + 4] = np.array([-1.0, 9.0, 9.0, -1.0]) / 16.0
    return made


def refine(haloed, planes, rows, width):
    along_y = rim_table(rows)
    empty = np.zeros((2 * rows, 5))
    along_y = np.concatenate([along_y[:, 1 : rows + 1], along_y[:, :1], along_y[:, rows + 1 :], empty], axis=1)
    both = np.kron(rim_table(1), along_y)
    both = jnp.asarray(np.concatenate([both, both], axis=1), jnp.bfloat16)
    return pl.pallas_call(
        refine_kernel,
        grid=(planes,),
        out_shape=jax.ShapeDtypeStruct((2 * planes, 2 * rows, width), jnp.float32),
        in_specs=[
            pl.BlockSpec(haloed.shape, lambda i: (0, 0, 0)),
            pl.BlockSpec(both.shape, lambda i: (0, 0)),
        ],
        out_specs=pl.BlockSpec((2, 2 * rows, width), lambda i: (i, 0, 0)),
        compiler_params=pltpu.CompilerParams(vmem_limit_bytes=16 * 1024 * 1024),
    )(haloed, both)


def per_device(charges, kernel):
    planes, rows, count = kernel.shape
    width = charges.shape[2]
    replicas = width // count
    half = replicas // 2
    blocks_z, blocks_y = lax.axis_size("gz"), lax.axis_size("gy")
    devices = blocks_z * blocks_y
    place = planes * rows
    fits = place == LANES and 2 * count == LANES and half == 8 and blocks_z == 8
    if not fits or count != CHUNKS * devices or replicas % 2 or rows % 8 or planes != 8 or devices % 8:
        return plain(charges, kernel)
    size = 2 * half
    per = LANES // size
    lines_x = pair_table(count, replicas, devices)
    table_x, table_f = [], []
    for chunk in range(CHUNKS):
        high, low = table(lines_x[chunk].reshape(devices // per, LANES, width))
        table_x.append(jnp.concatenate([high, low], axis=1).reshape(-1, width))
        table_f += table(refined(lines_x[chunk], 1).reshape(-1, 2 * width))
    table_y = table(y_table(count, planes, rows))
    tables = [*table_x, *table(line_table(count, devices)), *table_y, *z_tables(count, blocks_z), *table_f]
    deep = devices * size
    vmem = pl.BlockSpec(memory_space=pltpu.VMEM)
    block = lambda *shape: pltpu.VMEM(shape, jnp.float32)
    dma = pltpu.SemaphoreType.DMA
    stage = [block(planes, deep), block(2 * planes, deep), block(4, 8, deep)]
    rim = [
        block(rows, deep), block(2 * rows, deep), block(planes, deep), block(2 * planes, deep),
        block(4, 8, deep),
    ]
    haloed = pl.pallas_call(
        functools.partial(main_kernel, (count, blocks_z, blocks_y, half, len(tables))),
        out_shape=jax.ShapeDtypeStruct((planes + 3, rows + 8, 2 * width), jnp.float32),
        in_specs=[vmem, vmem] + [pl.BlockSpec(memory_space=pl.ANY)] * len(tables),
        out_specs=vmem,
        scratch_shapes=[
            *(pltpu.VMEM(t.shape, t.dtype) for t in tables),
            dma((len(tables),)), dma((CHUNKS, 2, devices)), dma((CHUNKS, 2, devices)), dma((CHUNKS, 2, 8)),
            block(devices * (size + 8), LANES), block(deep, LANES),
            block(devices * (size + 8), LANES), block(deep, LANES),
            block(deep, LANES), block(deep, LANES),
            block(deep, LANES), block(deep, LANES),
            block(place, deep), block(place, deep),
            *stage, *stage, *rim, *rim,
        ],
        compiler_params=pltpu.CompilerParams(
            collective_id=0, has_side_effects=True, vmem_limit_bytes=44 * 1024 * 1024
        ),
    )(charges.reshape(place, width), kernel.reshape(place, count), *tables)
    return refine(haloed, planes, rows, 2 * width)


def solution(mesh):
    placed = (P("gz", "gy", None), P("gz", "gy", None))
    return jax.shard_map(
        per_device, mesh=mesh, in_specs=placed, out_specs=P("gz", "gy", None), check_vma=False
    )
```

time: 65.8 us -> 66.7 us (1.014)
  local copies, waits for them, and re-layouts: 0 us -> 13.2 us
  Pallas kernels: 65.2 us -> 53 us
    unnamed x0 -> x24, local copies, waits for them, and re-layouts: none -> 13.2 us
    pallas_call x1, Pallas kernels: 57.7 us -> 48.4 us  [per_device(): pl.pallas_call(functools.partial(main_kernel, (count, blocks_z, blocks_y,...]
    pallas_call x1, Pallas kernels: 7.47 us -> 4.53 us  [refine(): pl.pallas_call(refine_kernel, grid=(planes,), out_shape=jax.ShapeDtypeStr...]
where the time goes in v1:
time: 66.7 us; the launch traced here: 66.2 us
  Pallas kernels  53 us (79%)
  local copies, waits for them, and re-layouts  13.2 us (20%)
    pallas_call x1, Pallas kernels, per_device(): pl.pallas_call(functools.partial(main_kernel, (count, blocks_z, blocks_y,...  48.4 us
    unnamed x24, local copies, waits for them, and re-layouts  13.2 us
    pallas_call x1, Pallas kernels, refine(): pl.pallas_call(refine_kernel, grid=(planes,), out_shape=jax.ShapeDtypeStr...  4.53 us

profile of v1, /device:TPU:0, one launch (start us, length us, event | category | flops | bytes accessed | tf_op | source)
XLA Modules:
  0.0 66.2 jit_solution(460302681750298560)
XLA Ops:
  0.0 0.0 copy-start.1
  0.0 1.6 %copy-done.1 = bf16[1024,1024]{1,0:T(8,128)(2,1)S(1)} copy-done((bf16[1024,1024]{1,0:T(8,128)(2,1)S(1)}, bf16[1024,1024]{1,0:T(8,128)(2,1)}, u32[]{:S(2)}) %copy-start.1) | copy-done | bytes 2097176
  1.6 0.0 copy-start.2
  1.6 1.6 %copy-done.2 = bf16[1024,1024]{1,0:T(8,128)(2,1)S(1)} copy-done((bf16[1024,1024]{1,0:T(8,128)(2,1)S(1)}, bf16[1024,1024]{1,0:T(8,128)(2,1)}, u32[]{:S(2)}) %copy-start.2) | copy-done | bytes 2097176
  3.2 0.0 copy-start.3
  3.2 1.6 %copy-done.3 = bf16[1024,1024]{1,0:T(8,128)(2,1)S(1)} copy-done((bf16[1024,1024]{1,0:T(8,128)(2,1)S(1)}, bf16[1024,1024]{1,0:T(8,128)(2,1)}, u32[]{:S(2)}) %copy-start.3) | copy-done | bytes 2097176
  4.8 0.0 copy-start.4
  4.8 1.6 %copy-done.4 = bf16[1024,1024]{1,0:T(8,128)(2,1)S(1)} copy-done((bf16[1024,1024]{1,0:T(8,128)(2,1)S(1)}, bf16[1024,1024]{1,0:T(8,128)(2,1)}, u32[]{:S(2)}) %copy-start.4) | copy-done | bytes 2097176
  6.4 0.0 copy-start.5
  6.4 1.0 %copy-done.5 = f32[8,16,1024]{2,1,0:T(8,128)S(1)} copy-done((f32[8,16,1024]{2,1,0:T(8,128)S(1)}, f32[8,16,1024]{2,1,0:T(8,128)}, u32[]{:S(2)}) %copy-start.5) | copy-done | bytes 524312
  7.4 0.0 copy-start.6
  7.4 0.8 %copy-done.6 = f32[8,16,64]{2,1,0:T(8,128)S(1)} copy-done((f32[8,16,64]{2,1,0:T(8,128)S(1)}, f32[8,16,64]{2,1,0:T(8,128)}, u32[]{:S(2)}) %copy-start.6) | copy-done | bytes 32792
  8.2 0.0 copy-start.7
  8.3 0.8 %copy-done.7 = bf16[128,192]{1,0:T(8,128)(2,1)S(1)} copy-done((bf16[128,192]{1,0:T(8,128)(2,1)S(1)}, bf16[128,192]{1,0:T(8,128)(2,1)}, u32[]{:S(2)}) %copy-start.7) | copy-done | bytes 49176
  9.1 0.0 copy-start.8
  9.1 0.8 %copy-done.8 = bf16[128,192]{1,0:T(8,128)(2,1)S(1)} copy-done((bf16[128,192]{1,0:T(8,128)(2,1)S(1)}, bf16[128,192]{1,0:T(8,128)(2,1)}, u32[]{:S(2)}) %copy-start.8) | copy-done | bytes 49176
  9.9 0.0 copy-start.9
  9.9 0.8 %copy-done.9 = bf16[256,64]{1,0:T(8,128)(2,1)S(1)} copy-done((bf16[256,64]{1,0:T(8,128)(2,1)S(1)}, bf16[256,64]{1,0:T(8,128)(2,1)}, u32[]{:S(2)}) %copy-start.9) | copy-done | bytes 32792
  10.8 0.0 copy-start.10
  10.8 0.8 %copy-done.10 = bf16[256,64]{1,0:T(8,128)(2,1)S(1)} copy-done((bf16[256,64]{1,0:T(8,128)(2,1)S(1)}, bf16[256,64]{1,0:T(8,128)(2,1)}, u32[]{:S(2)}) %copy-start.10) | copy-done | bytes 32792
  11.6 0.0 copy-start.11
  11.6 48.4 %shard_map.163.x_ref = f32[11,24,2048]{2,1,0:T(8,128)} custom-call(f32[128,1024]{1,0:T(8,128)S(1)} %bitcast.2, f32[128,64]{1,0:T(8,128)S(1)} %bitcast.3, bf16[1024,1024]{1,0:T(8,128)(2,1)S(1)} %copy-done.2, bf16[1024,1024]{1,0:T(8,128)(2,1)S(1)} %copy-done.1, bf16[256,64]{1,0:T(8,128)(2,1)S(1)} %copy-done.10, bf16[256,64]{1,0:T(8,128)(2,1)S(1)} %copy-done.9, ...), custom_call_target="tpu_custom_call" | custom-call | tf_op jit(solution)/shard_map/pallas_call | solution.py:569
  60.0 0.0 copy-done.11
  60.1 0.0 copy-start
  60.1 1.6 %copy-done = f32[11,24,2048]{2,1,0:T(8,128)S(1)} copy-done((f32[11,24,2048]{2,1,0:T(8,128)S(1)}, f32[11,24,2048]{2,1,0:T(8,128)}, u32[]{:S(2)}) %copy-start) | copy-done | bytes 2162712
  61.7 4.5 %shard_map.164 = f32[16,32,2048]{2,1,0:T(8,128)} custom-call(f32[11,24,2048]{2,1,0:T(8,128)S(1)} %copy-done, bf16[64,192]{1,0:T(8,128)(2,1)S(1)} %copy-done.11), custom_call_target="tpu_custom_call" | custom-call | tf_op jit(solution)/shard_map/pallas_call | solution.py:526
Async XLA Ops:
  0.0 1.6 %copy-start.1 = (bf16[1024,1024]{1,0:T(8,128)(2,1)S(1)}, bf16[1024,1024]{1,0:T(8,128)(2,1)}, u32[]{:S(2)}) copy-start(bf16[1024,1024]{1,0:T(8,128)(2,1)} %constant.48.refs_3_) | copy-start | bytes 6291460
  1.6 1.6 %copy-start.2 = (bf16[1024,1024]{1,0:T(8,128)(2,1)S(1)}, bf16[1024,1024]{1,0:T(8,128)(2,1)}, u32[]{:S(2)}) copy-start(bf16[1024,1024]{1,0:T(8,128)(2,1)} %constant.46.refs_2_) | copy-start | bytes 6291460
  3.2 1.6 %copy-start.3 = (bf16[1024,1024]{1,0:T(8,128)(2,1)S(1)}, bf16[1024,1024]{1,0:T(8,128)(2,1)}, u32[]{:S(2)}) copy-start(bf16[1024,1024]{1,0:T(8,128)(2,1)} %constant.39.clone.refs_7_) | copy-start | bytes 6291460
  4.8 1.6 %copy-start.4 = (bf16[1024,1024]{1,0:T(8,128)(2,1)S(1)}, bf16[1024,1024]{1,0:T(8,128)(2,1)}, u32[]{:S(2)}) copy-start(bf16[1024,1024]{1,0:T(8,128)(2,1)} %constant.38.clone.refs_6_) | copy-start | bytes 6291460
  6.4 1.0 %copy-start.5 = (f32[8,16,1024]{2,1,0:T(8,128)S(1)}, f32[8,16,1024]{2,1,0:T(8,128)}, u32[]{:S(2)}) copy-start(f32[8,16,1024]{2,1,0:T(8,128)} %param.17) | copy-start | bytes 1572868
  7.4 0.8 %copy-start.6 = (f32[8,16,64]{2,1,0:T(8,128)S(1)}, f32[8,16,64]{2,1,0:T(8,128)}, u32[]{:S(2)}) copy-start(f32[8,16,64]{2,1,0:T(8,128)} %param.18) | copy-start | bytes 98308
  8.2 0.8 %copy-start.7 = (bf16[128,192]{1,0:T(8,128)(2,1)S(1)}, bf16[128,192]{1,0:T(8,128)(2,1)}, u32[]{:S(2)}) copy-start(bf16[128,192]{1,0:T(8,128)(2,1)} %constant.43.clone.refs_9_) | copy-start | bytes 147460
  9.1 0.8 %copy-start.8 = (bf16[128,192]{1,0:T(8,128)(2,1)S(1)}, bf16[128,192]{1,0:T(8,128)(2,1)}, u32[]{:S(2)}) copy-start(bf16[128,192]{1,0:T(8,128)(2,1)} %constant.42.clone.refs_8_) | copy-start | bytes 147460
  9.9 0.8 %copy-start.9 = (bf16[256,64]{1,0:T(8,128)(2,1)S(1)}, bf16[256,64]{1,0:T(8,128)(2,1)}, u32[]{:S(2)}) copy-start(bf16[256,64]{1,0:T(8,128)(2,1)} %constant.41.clone.refs_5_) | copy-start | bytes 98308
  10.8 0.8 %copy-start.10 = (bf16[256,64]{1,0:T(8,128)(2,1)S(1)}, bf16[256,64]{1,0:T(8,128)(2,1)}, u32[]{:S(2)}) copy-start(bf16[256,64]{1,0:T(8,128)(2,1)} %constant.40.clone.refs_4_) | copy-start | bytes 98308
  11.6 48.4 %copy-start.11 = (bf16[64,192]{1,0:T(8,128)(2,1)S(1)}, bf16[64,192]{1,0:T(8,128)(2,1)}, u32[]{:S(2)}) copy-start(bf16[64,192]{1,0:T(8,128)(2,1)} %constant.44.clone.r_ref) | copy-start | bytes 73732
  60.1 1.6 %copy-start = (f32[11,24,2048]{2,1,0:T(8,128)S(1)}, f32[11,24,2048]{2,1,0:T(8,128)}, u32[]{:S(2)}) copy-start(f32[11,24,2048]{2,1,0:T(8,128)} %shard_map.163.x_ref) | copy-start | bytes 6488068

commit v2 on v1

--- a/solution.py
+++ b/solution.py
@@ -449,56 +449,80 @@
                 at = (group * per + inner) * step
                 sent[chunk][at : at + size, :] = made[inner * size : (inner + 1) * size, :]
 
-    loads[2].wait()
-    loads[3].wait()
-    lines = mul3((table_k[0][...], table_k[1][...]), split(k_ref[...]), ((1,), (1,)))
-    for device in range(devices):
-        sent[0][device * pitch + size : device * pitch + size + 8, :] = lines[device * 8 : (device + 1) * 8, :]
-    loads[0].wait()
-    x_lines(0)
-    pl.semaphore_wait(barrier, devices - 1)
-    there = [exchange(blocks_z, blocks_y, size + 2, sent[0], held[0], sent_sem.at[0])]
-    loads[1].wait()
-    x_lines(1)
-    there.append(exchange(blocks_z, blocks_y, size, sent[1], held[1], sent_sem.at[1]))
-    for load in loads[4:8]:
-        load.wait()
+    scope = jax.named_scope
+    with scope("kernel_lines"):
+        loads[2].wait()
+        loads[3].wait()
+        lines = mul3((table_k[0][...], table_k[1][...]), split(k_ref[...]), ((1,), (1,)))
+        for device in range(devices):
+            at = device * pitch + size
+            sent[0][at : at + 8, :] = lines[device * 8 : (device + 1) * 8, :]
+    with scope("x_load"):
+        loads[0].wait()
+    with scope("x_lines0"):
+        x_lines(0)
+    with scope("barrier"):
+        pl.semaphore_wait(barrier, devices - 1)
+    with scope("send0"):
+        there = [exchange(blocks_z, blocks_y, size + 2, sent[0], held[0], sent_sem.at[0])]
+    with scope("x_lines1"):
+        loads[1].wait()
+        x_lines(1)
+    with scope("send1"):
+        there.append(exchange(blocks_z, blocks_y, size, sent[1], held[1], sent_sem.at[1]))
+    with scope("wait_there0"):
+        for load in loads[4:8]:
+            load.wait()
+        wait_recv(there[0])
     y_pair = (table_y[0][...], table_y[1][...])
+    z_pair = (table_z[0][...], table_z[1][...])
     shape = (count, blocks_z, blocks_y, half)
-    wait_recv(there[0])
-    green = middle_stage(shape, held[0], y_pair, table_z[0][...], table_z[1][...], None, back[0])
-    returns = [exchange(blocks_z, blocks_y, size, back[0], home[0], back_sem.at[0])]
-    wait_recv(there[1])
-    middle_stage(shape, held[1], y_pair, table_z[0][...], table_z[1][...], green[:, LANES:], back[1])
-    returns.append(exchange(blocks_z, blocks_y, size, back[1], home[1], back_sem.at[1]))
+    with scope("middle0"):
+        green = middle_stage(shape, held[0], y_pair, *z_pair, None, back[0])
+    with scope("return0"):
+        returns = [exchange(blocks_z, blocks_y, size, back[0], home[0], back_sem.at[0])]
+    with scope("wait_there1"):
+        wait_recv(there[1])
+    with scope("middle1"):
+        middle_stage(shape, held[1], y_pair, *z_pair, green[:, LANES:], back[1])
+    with scope("return1"):
+        returns.append(exchange(blocks_z, blocks_y, size, back[1], home[1], back_sem.at[1]))
     for load in loads[8:]:
         load.wait()
     borders = []
     for chunk in range(CHUNKS):
         fine = (table_f[2 * chunk][...], table_f[2 * chunk + 1][...])
-        wait_recv(returns[chunk])
-        turned = jnp.transpose(home[chunk][...])
-        own[chunk][...] = turned
-        borders.append(
-            send_rims(blocks_z, blocks_y, planes, rows, own[chunk], stages[chunk], rims[chunk], rim_sem.at[chunk])
-        )
-        made = mul3(split(turned), fine).reshape(planes, rows, -1)
-        if chunk:
-            made = out[1 : planes + 1, :rows, :] + made
-        out[1 : planes + 1, :rows, :] = made
-        wait_recv(borders[chunk])
-        made = mul3(split(rim_lines(planes, rims[chunk])), fine)
-        deep = 3 * rows
-        ends, sides = made[:deep].reshape(3, rows, -1), made[deep:].reshape(planes + 3, 8, -1)
-        if chunk:
-            sides = out[:, rows:, :] + sides
-            ends = jnp.concatenate([out[0:1, :rows, :], out[planes + 1 :, :rows, :]], axis=0) + ends
-        out[:, rows:, :] = sides
-        out[0:1, :rows, :] = ends[0:1]
-        out[planes + 1 :, :rows, :] = ends[1:]
-    for copies in there + returns + borders:
-        for copy in copies:
-            copy.wait_send()
+        with scope(f"wait_back{chunk}"):
+            wait_recv(returns[chunk])
+        with scope(f"turn{chunk}"):
+            turned = jnp.transpose(home[chunk][...])
+            own[chunk][...] = turned
+        with scope(f"send_rim{chunk}"):
+            borders.append(send_rims(
+                blocks_z, blocks_y, planes, rows, own[chunk], stages[chunk], rims[chunk], rim_sem.at[chunk]
+            ))
+        with scope(f"own{chunk}"):
+            made = mul3(split(turned), fine).reshape(planes, rows, -1)
+            if chunk:
+                made = out[1 : planes + 1, :rows, :] + made
+            out[1 : planes + 1, :rows, :] = made
+        with scope(f"wait_rim{chunk}"):
+            wait_recv(borders[chunk])
+        with scope(f"rim{chunk}"):
+            made = mul3(split(rim_lines(planes, rims[chunk])), fine)
+            deep = 3 * rows
+            ends, sides = made[:deep].reshape(3, rows, -1), made[deep:].reshape(planes + 3, 8, -1)
+            if chunk:
+                sides = out[:, rows:, :] + sides
+                held_ends = [out[0:1, :rows, :], out[planes + 1 :, :rows, :]]
+                ends = jnp.concatenate(held_ends, axis=0) + ends
+            out[:, rows:, :] = sides
+            out[0:1, :rows, :] = ends[0:1]
+            out[planes + 1 :, :rows, :] = ends[1:]
+    with scope("wait_sends"):
+        for copies in there + returns + borders:
+            for copy in copies:
+                copy.wait_send()
 
 
 def refine_kernel(x_ref, r_ref, o_ref):
@@ -532,7 +556,6 @@
             pl.BlockSpec(both.shape, lambda i: (0, 0)),
         ],
         out_specs=pl.BlockSpec((2, 2 * rows, width), lambda i: (i, 0, 0)),
-        compiler_params=pltpu.CompilerParams(vmem_limit_bytes=16 * 1024 * 1024),
     )(haloed, both)
 
 
@@ -582,7 +605,7 @@
             *stage, *stage, *rim, *rim,
         ],
         compiler_params=pltpu.CompilerParams(
-            collective_id=0, has_side_effects=True, vmem_limit_bytes=44 * 1024 * 1024
+            collective_id=0, has_side_effects=True, vmem_limit_bytes=60 * 1024 * 1024
         ),
     )(charges.reshape(place, width), kernel.reshape(place, count), *tables)
     return refine(haloed, planes, rows, 2 * width)

time: 66.7 us -> 55.2 us (0.83)
  local copies, waits for them, and re-layouts: 13.2 us -> 0 us
  Pallas kernels: 53 us -> 55 us
    unnamed x24 -> x0, local copies, waits for them, and re-layouts: 13.2 us -> none
    pallas_call x1, Pallas kernels: 4.53 us -> 6.17 us  [refine(): pl.pallas_call(refine_kernel, grid=(planes,), out_shape=jax.ShapeDtypeStr...]
where the time goes in v2:
time: 55.2 us; the launch traced here: 55.1 us
  Pallas kernels  55 us (100%)
    pallas_call x1, Pallas kernels, per_device(): pl.pallas_call(functools.partial(main_kernel, (count, blocks_z, blocks_y,...  48.9 us
    pallas_call x1, Pallas kernels, refine(): pl.pallas_call(refine_kernel, grid=(planes,), out_shape=jax.ShapeDtypeStr...  6.17 us

profile of v2, /device:TPU:0, one launch (start us, length us, event | category | flops | bytes accessed | tf_op | source)
XLA Modules:
  0.0 55.1 jit_solution(16755074709666021801)
XLA Ops:
  0.0 48.9 %shard_map.163.x_ref = f32[11,24,2048]{2,1,0:T(8,128)} custom-call(f32[128,1024]{1,0:T(8,128)} %bitcast.2, f32[128,64]{1,0:T(8,128)} %bitcast.3, bf16[1024,1024]{1,0:T(8,128)(2,1)} %constant.46.refs_2_, bf16[1024,1024]{1,0:T(8,128)(2,1)} %constant.48.refs_3_, bf16[256,64]{1,0:T(8,128)(2,1)} %constant.40.clone.refs_4_, ...), custom_call_target="tpu_custom_call" | custom-call | tf_op jit(solution)/shard_map/pallas_call | solution.py:592
  48.9 6.2 %shard_map.164 = f32[16,32,2048]{2,1,0:T(8,128)} custom-call(f32[11,24,2048]{2,1,0:T(8,128)} %shard_map.163.x_ref, bf16[64,192]{1,0:T(8,128)(2,1)} %constant.44.clone.r_ref), custom_call_target="tpu_custom_call" | custom-call | tf_op jit(solution)/shard_map/pallas_call | solution.py:550

commit v3 on v2

--- a/solution.py
+++ b/solution.py
@@ -185,6 +185,13 @@
 CHUNKS = 2
 
 
+def mul3_rows(left, right):
+    (a, b), (c, d) = left, right
+    rows = a.shape[0]
+    both = mul(jnp.concatenate([b, a], axis=0), c)
+    return mul(a, d) + both[:rows] + both[rows:]
+
+
 def line_of(device, chunk, count):
     flip = np.where(device == 0, count // 2, (count - device) % count)
     return np.where(chunk == 0, device, flip)
@@ -225,45 +232,43 @@
     return forward, inverse
 
 
-def remote(source, target, sems, number, place):
-    copy = pltpu.make_async_remote_copy(
-        src_ref=source, dst_ref=target, send_sem=sems.at[0, number], recv_sem=sems.at[1, number],
+def remote(source, target, sems, place):
+    return pltpu.make_async_remote_copy(
+        src_ref=source, dst_ref=target, send_sem=sems.at[0], recv_sem=sems.at[1],
         device_id=place, device_id_type=MESH,
     )
-    copy.start()
-    return copy
 
 
 def exchange(blocks_z, blocks_y, rows, source, target, sems):
     size = blocks_z * blocks_y // GROUPS
+    devices = size * GROUPS
     me = lax.axis_index("gz") * blocks_y + lax.axis_index("gy")
     group, inner = me // size, lax.rem(me, size)
     high, low = group // 2, lax.rem(group, 2)
-    pitch_from, pitch_to = source.shape[0] // (size * GROUPS), target.shape[0] // (size * GROUPS)
-
-    def span(ref, device, pitch):
-        return ref.at[pl.ds(pl.multiple_of(device * pitch, 8), rows)]
-
-    copies = []
+    turn = lax.rem(high + low, 2)
+    pitch_from, pitch_to = source.shape[0] // devices, target.shape[0] // devices
+
     for flip_high, flip_low in ((1, 0), (1, 1), (0, 1), (0, 0)):
-        other_group = lax.rem(high + flip_high, 2) * 2 + lax.rem(low + flip_low, 2)
+        far = lax.rem(high + flip_high + turn, 2) * 2 + lax.rem(low + flip_low + turn, 2)
         for step in range(size):
-            if (flip_high, flip_low, step) == (0, 0, 0):
-                continue
-            other = other_group * size + lax.rem(inner + step, size)
-            copies.append(remote(
-                span(source, other, pitch_from), span(target, me, pitch_to), sems, len(copies),
-                (other // blocks_y, lax.rem(other, blocks_y)),
-            ))
-    mine_from = pl.ds(pl.multiple_of(me * pitch_from, 8), min(pitch_from, pitch_to))
-    mine_to = pl.ds(pl.multiple_of(me * pitch_to, 8), min(pitch_from, pitch_to))
-    target[mine_to, :] = source[mine_from, :]
-    return copies
-
-
-def wait_recv(copies):
-    for copy in copies:
-        copy.wait_recv()
+            other = far * size + lax.rem(inner + step, size)
+            there = remote(
+                source.at[pl.ds(pl.multiple_of(other * pitch_from, 8), rows)],
+                target.at[pl.ds(pl.multiple_of(me * pitch_to, 8), rows)],
+                sems, (other // blocks_y, lax.rem(other, blocks_y)),
+            )
+            if step == 0 and flip_high == flip_low:
+                pl.when(other != me)(there.start)
+            else:
+                there.start()
+    span = min(pitch_from, pitch_to)
+    mine_from = pl.ds(pl.multiple_of(me * pitch_from, 8), span)
+    target[pl.ds(pl.multiple_of(me * pitch_to, 8), span), :] = source[mine_from, :]
+    other = lax.rem(me + 1, devices)
+    count = pl.ds(0, (devices - 1) * rows)
+    return remote(
+        source.at[count], target.at[count], sems, (other // blocks_y, lax.rem(other, blocks_y))
+    )
 
 
 def swap_parts(values):
@@ -287,7 +292,7 @@
     return ref[pl.ds(start, blocks, stride=stride), :]
 
 
-def middle_stage(sizes, held, table_y, forward, inverse, green, back):
+def middle_stage(sizes, held, table_y, table_b, forward, inverse, green, back):
     count, blocks_z, blocks_y, half = sizes
     planes = count // blocks_z
     pitch = held.shape[0] // (blocks_z * blocks_y)
@@ -310,7 +315,7 @@
             jnp.concatenate([keep * first + (1.0 - keep) * second, -keep * second], axis=1)
         )
     width = len(lines)
-    data = mul3(split(jnp.concatenate(lines, axis=0)), table_y)
+    data = mul3_rows(split(jnp.concatenate(lines, axis=0)), table_y)
     data = jnp.concatenate(
         [
             jnp.concatenate(
@@ -350,7 +355,7 @@
         ],
         axis=0,
     )
-    data = mul3(split(data), table_y, ((1,), (1,)))
+    data = mul3_rows(split(data), table_b)
     out_pitch = 2 * half
     for column in range(half):
         for part in range(2):
@@ -362,17 +367,13 @@
     return spectra
 
 
-def send_rims(blocks_z, blocks_y, planes, rows, own, stage, rims, sems):
+def send_rims(blocks_z, blocks_y, planes, rows, own, sizes, stage, rims, sems):
     to_up, to_down, to_corner = stage
     low_z, high_z, low_y, high_y, corner = rims
     gz, gy = lax.axis_index("gz"), lax.axis_index("gy")
     next_z, last_z = lax.rem(gz + 1, blocks_z), lax.rem(gz + blocks_z - 1, blocks_z)
     next_y, last_y = lax.rem(gy + 1, blocks_y), lax.rem(gy + blocks_y - 1, blocks_y)
     end = (planes - 1) * rows
-    copies = [
-        remote(own.at[pl.ds(0, 2 * rows)], high_z, sems, 0, (last_z, gy)),
-        remote(own.at[pl.ds(end, rows)], low_z, sems, 1, (next_z, gy)),
-    ]
     def side(row):
         return jnp.concatenate([own[p * rows + row : p * rows + row + 1, :] for p in range(planes)], axis=0)
 
@@ -385,15 +386,27 @@
         pieces = [own[r : r + 1, :] for r in pick]
         pieces.append(jnp.zeros((8 - len(pick), own.shape[1]), jnp.float32))
         to_corner[number] = jnp.concatenate(pieces, axis=0)
-    copies.append(remote(to_down, high_y, sems, 2, (gz, last_y)))
-    copies.append(remote(to_up, low_y, sems, 3, (gz, next_y)))
     places = ((next_z, next_y), (next_z, last_y), (last_z, next_y), (last_z, last_y))
+    copies = []
     for number, (pick, place) in enumerate(zip(picks, places)):
         span = pl.ds(0, len(pick))
         copies.append(
-            remote(to_corner.at[number, span], corner.at[number, span], sems, 4 + number, place)
+            remote(to_corner.at[number, span], corner.at[number, span], sems, place)
         )
-    return copies
+    for copy in copies:
+        copy.start()
+    down = remote(own.at[pl.ds(0, 2 * rows)], high_z, sems, (last_z, gy))
+    up = remote(own.at[pl.ds(end, rows)], low_z, sems, (next_z, gy))
+    pl.when(gz == 0)(down.start)
+    up.start()
+    pl.when(gz != 0)(down.start)
+    sides = [
+        remote(to_up, low_y, sems, (gz, next_y)), remote(to_down, high_y, sems, (gz, last_y)),
+    ]
+    for copy in sides:
+        copy.start()
+    count = pl.ds(0, 3 * (planes + rows + 3) * own.shape[1] // LANES)
+    return remote(sizes[0].at[count], sizes[1].at[count], sems, (next_z, gy))
 
 
 def rim_lines(planes, rims):
@@ -406,6 +419,7 @@
         ]
     tiles += [corner[2, 0:1, :], corner[3, 0:2, :], empty]
     tiles += [corner[2, 1:2, :], corner[3, 2:4, :], empty]
+    tiles += [jnp.zeros((8, low_z.shape[1]), jnp.float32)]
     return jnp.concatenate([low_z[...], high_z[...], *tiles], axis=0)
 
 
@@ -413,20 +427,17 @@
     count, blocks_z, blocks_y, half, n_tables = sizes
     devices = blocks_z * blocks_y
     planes = count // blocks_z
-    q_ref, k_ref = refs[:2]
-    sources = refs[2 : 2 + n_tables]
+    sources = refs[: 2 + n_tables]
     out = refs[2 + n_tables]
-    tables = refs[3 + n_tables : 3 + 2 * n_tables]
-    rest = list(refs[3 + 2 * n_tables :])
-    table_sem, sent_sem, back_sem, rim_sem = rest[:4]
-    sent, held, back, home, own = (rest[4 + 2 * i : 6 + 2 * i] for i in range(5))
-    stages, rims = (rest[14:17], rest[17:20]), (rest[20:25], rest[25:30])
-    table_x, table_k, table_y, table_z, table_f = (
-        tables[0:2], tables[2:4], tables[4:6], tables[6:8], tables[8:12]
-    )
-    loads = [pltpu.make_async_copy(s, t, table_sem.at[i]) for i, (s, t) in enumerate(zip(sources, tables))]
-    for load in loads:
-        load.start()
+    loaded = refs[3 + n_tables : 5 + 2 * n_tables]
+    (q_ref, k_ref), tables = loaded[:2], loaded[2:]
+    rest = list(refs[5 + 2 * n_tables :])
+    load_sem, sent_sem, back_sem, rim_sem, out_sem, total, packed = rest[:7]
+    sent, held, back, home, own = (rest[7 + 2 * i : 9 + 2 * i] for i in range(5))
+    stages, rims = (rest[17:20], rest[20:23]), (rest[23:28], rest[28:33])
+    table_k, table_x, table_y, table_b, table_z, table_f = (
+        tables[0:2], tables[2:4], tables[4:6], tables[6:8], tables[8:10], tables[10:14]
+    )
     me = lax.axis_index("gz") * blocks_y + lax.axis_index("gy")
     barrier = pltpu.get_barrier_semaphore()
     for step in range(1, devices):
@@ -434,12 +445,16 @@
         pl.semaphore_signal(
             barrier, inc=1, device_id=(other // blocks_y, lax.rem(other, blocks_y)), device_id_type=MESH
         )
+    loads = [
+        pltpu.make_async_copy(s, t, load_sem.at[i]) for i, (s, t) in enumerate(zip(sources, loaded))
+    ]
+    for load in loads[:5]:
+        load.start()
     rows = q_ref.shape[0] // planes
     size = 2 * half
-    charges = jnp.concatenate(split(q_ref[...]), axis=0)
     pitch = sent[0].shape[0] // devices
 
-    def x_lines(chunk):
+    def x_lines(chunk, charges):
         per = LANES // size
         for group in range(devices // per):
             both = mul(table_x[chunk][group * 2 * LANES : (group + 1) * 2 * LANES, :], charges, ((1,), (1,)))
@@ -451,86 +466,130 @@
 
     scope = jax.named_scope
     with scope("kernel_lines"):
-        loads[2].wait()
-        loads[3].wait()
+        for load in loads[1:4]:
+            load.wait()
         lines = mul3((table_k[0][...], table_k[1][...]), split(k_ref[...]), ((1,), (1,)))
         for device in range(devices):
             at = device * pitch + size
             sent[0][at : at + 8, :] = lines[device * 8 : (device + 1) * 8, :]
     with scope("x_load"):
         loads[0].wait()
+        loads[4].wait()
+        for load in loads[5:]:
+            load.start()
     with scope("x_lines0"):
-        x_lines(0)
+        charges = jnp.concatenate(split(q_ref[...]), axis=0)
+        x_lines(0, charges)
     with scope("barrier"):
         pl.semaphore_wait(barrier, devices - 1)
     with scope("send0"):
         there = [exchange(blocks_z, blocks_y, size + 2, sent[0], held[0], sent_sem.at[0])]
     with scope("x_lines1"):
-        loads[1].wait()
-        x_lines(1)
+        loads[5].wait()
+        x_lines(1, charges)
     with scope("send1"):
         there.append(exchange(blocks_z, blocks_y, size, sent[1], held[1], sent_sem.at[1]))
     with scope("wait_there0"):
-        for load in loads[4:8]:
+        for load in loads[6:12]:
             load.wait()
-        wait_recv(there[0])
-    y_pair = (table_y[0][...], table_y[1][...])
+        there[0].wait_recv()
+    y_pairs = ((table_y[0][...], table_y[1][...]), (table_b[0][...], table_b[1][...]))
     z_pair = (table_z[0][...], table_z[1][...])
     shape = (count, blocks_z, blocks_y, half)
     with scope("middle0"):
-        green = middle_stage(shape, held[0], y_pair, *z_pair, None, back[0])
+        green = middle_stage(shape, held[0], *y_pairs, *z_pair, None, back[0])
     with scope("return0"):
         returns = [exchange(blocks_z, blocks_y, size, back[0], home[0], back_sem.at[0])]
     with scope("wait_there1"):
-        wait_recv(there[1])
+        there[1].wait_recv()
     with scope("middle1"):
-        middle_stage(shape, held[1], y_pair, *z_pair, green[:, LANES:], back[1])
+        middle_stage(shape, held[1], *y_pairs, *z_pair, green[:, LANES:], back[1])
     with scope("return1"):
         returns.append(exchange(blocks_z, blocks_y, size, back[1], home[1], back_sem.at[1]))
-    for load in loads[8:]:
+    for load in loads[12:]:
         load.wait()
     borders = []
+    fine = [(table_f[2 * c][...], table_f[2 * c + 1][...]) for c in range(CHUNKS)]
     for chunk in range(CHUNKS):
-        fine = (table_f[2 * chunk][...], table_f[2 * chunk + 1][...])
         with scope(f"wait_back{chunk}"):
-            wait_recv(returns[chunk])
+            returns[chunk].wait_recv()
         with scope(f"turn{chunk}"):
             turned = jnp.transpose(home[chunk][...])
             own[chunk][...] = turned
         with scope(f"send_rim{chunk}"):
             borders.append(send_rims(
-                blocks_z, blocks_y, planes, rows, own[chunk], stages[chunk], rims[chunk], rim_sem.at[chunk]
+                blocks_z, blocks_y, planes, rows, own[chunk], home, stages[chunk], rims[chunk], rim_sem.at[chunk]
             ))
         with scope(f"own{chunk}"):
-            made = mul3(split(turned), fine).reshape(planes, rows, -1)
+            made = mul3_rows(split(turned), fine[chunk]).reshape(planes, rows, -1)
             if chunk:
-                made = out[1 : planes + 1, :rows, :] + made
-            out[1 : planes + 1, :rows, :] = made
+                made = total[1 : planes + 1, :rows, :] + made
+            total[1 : planes + 1, :rows, :] = made
+    flat = 3 * rows
+
+    def pack_own(first, last):
+        values = total[first:last, :rows, :]
+        high, low = split(values)
+        packed[first:last, :rows, :] = high
+        packed[first:last, rows : 2 * rows, :] = low
+
+    pack_own(1, planes + 1)
+    inside, around = (pl.ds(1, planes), pl.ds(0, 2 * rows)), (pl.ds(0, planes + 3), pl.ds(2 * rows, 16))
+    first, last = (pl.ds(0, 1), pl.ds(0, 2 * rows)), (pl.ds(planes + 1, 2), pl.ds(0, 2 * rows))
+    stores = [
+        pltpu.make_async_copy(packed.at[span], out.at[span], out_sem.at[i])
+        for i, span in enumerate((inside, around, first, last))
+    ]
+    stores[0].start()
+    for chunk in range(CHUNKS):
         with scope(f"wait_rim{chunk}"):
-            wait_recv(borders[chunk])
+            borders[chunk].wait_recv()
         with scope(f"rim{chunk}"):
-            made = mul3(split(rim_lines(planes, rims[chunk])), fine)
-            deep = 3 * rows
-            ends, sides = made[:deep].reshape(3, rows, -1), made[deep:].reshape(planes + 3, 8, -1)
-            if chunk:
-                sides = out[:, rows:, :] + sides
-                held_ends = [out[0:1, :rows, :], out[planes + 1 :, :rows, :]]
-                ends = jnp.concatenate(held_ends, axis=0) + ends
-            out[:, rows:, :] = sides
-            out[0:1, :rows, :] = ends[0:1]
-            out[planes + 1 :, :rows, :] = ends[1:]
+            made = mul3_rows(split(rim_lines(planes, rims[chunk])), fine[chunk])
+            sides = 8 * (planes + 3)
+            ends = made[:flat].reshape(3, rows, -1)
+            sides = made[flat : flat + sides].reshape(planes + 3, 8, -1)
+            if not chunk:
+                total[:, rows:, :] = sides
+                total[0:1, :rows, :] = ends[0:1]
+                total[planes + 1 :, :rows, :] = ends[1:]
+                continue
+            sides = total[:, rows:, :] + sides
+            high = sides.astype(jnp.bfloat16).astype(jnp.float32)
+            packed[:, 2 * rows :, :] = jnp.concatenate([high, sides - high], axis=1).astype(jnp.bfloat16)
+            stores[1].start()
+            for i, place in enumerate((0, planes + 1, planes + 2)):
+                high, low = split(total[place, :rows, :] + ends[i])
+                packed[place, :rows, :] = high
+                packed[place, rows : 2 * rows, :] = low
+    for store in stores[2:]:
+        store.start()
     with scope("wait_sends"):
-        for copies in there + returns + borders:
-            for copy in copies:
-                copy.wait_send()
-
-
-def refine_kernel(x_ref, r_ref, o_ref):
-    step = pl.program_id(0)
-    near = x_ref[pl.ds(step, 4)].reshape(4 * x_ref.shape[1], x_ref.shape[2])
-    high, low = split(near)
-    fine = mul(r_ref[...], jnp.concatenate([low, high], axis=0))
-    o_ref[...] = fine.reshape(o_ref.shape)
+        for copy in there + returns + borders:
+            copy.wait_send()
+        for store in stores:
+            store.wait()
+
+
+def refine_kernel(x_ref, r_ref, o_ref, held, made, sem, out_sem):
+    planes = x_ref.shape[0] - 3
+    loads = [
+        pltpu.make_async_copy(x_ref.at[p], held.at[p], sem.at[p]) for p in range(planes + 3)
+    ]
+    for load in loads:
+        load.start()
+    for load in loads[:3]:
+        load.wait()
+    stores = []
+    for p in range(planes):
+        loads[p + 3].wait()
+        near = held[p : p + 4].reshape(4 * held.shape[1], held.shape[2])
+        made[2 * p : 2 * p + 2] = mul(r_ref[...], near).reshape(2, -1, made.shape[2])
+        span = pl.ds(2 * p, 2)
+        stores.append(pltpu.make_async_copy(made.at[span], o_ref.at[span], out_sem.at[p]))
+        stores[-1].start()
+    for store in stores:
+        store.wait()
 
 
 def rim_table(count):
@@ -543,19 +602,23 @@
 
 def refine(haloed, planes, rows, width):
     along_y = rim_table(rows)
-    empty = np.zeros((2 * rows, 5))
-    along_y = np.concatenate([along_y[:, 1 : rows + 1], along_y[:, :1], along_y[:, rows + 1 :], empty], axis=1)
-    both = np.kron(rim_table(1), along_y)
-    both = jnp.asarray(np.concatenate([both, both], axis=1), jnp.bfloat16)
+    middle = along_y[:, 1 : rows + 1]
+    sides = np.concatenate([along_y[:, :1], along_y[:, rows + 1 :], np.zeros((2 * rows, 5))], axis=1)
+    along_y = np.concatenate([middle, middle, sides, sides], axis=1)
+    both = jnp.asarray(np.kron(rim_table(1), along_y), jnp.bfloat16)
+    shape = (2 * planes, 2 * rows, width)
     return pl.pallas_call(
         refine_kernel,
-        grid=(planes,),
-        out_shape=jax.ShapeDtypeStruct((2 * planes, 2 * rows, width), jnp.float32),
+        out_shape=jax.ShapeDtypeStruct(shape, jnp.float32),
         in_specs=[
-            pl.BlockSpec(haloed.shape, lambda i: (0, 0, 0)),
-            pl.BlockSpec(both.shape, lambda i: (0, 0)),
+            pl.BlockSpec(memory_space=pl.ANY),
+            pl.BlockSpec(memory_space=pltpu.VMEM),
         ],
-        out_specs=pl.BlockSpec((2, 2 * rows, width), lambda i: (i, 0, 0)),
+        out_specs=pl.BlockSpec(memory_space=pl.ANY),
+        scratch_shapes=[
+            pltpu.VMEM(haloed.shape, haloed.dtype), pltpu.VMEM(shape, jnp.float32),
+            pltpu.SemaphoreType.DMA((planes + 3,)), pltpu.SemaphoreType.DMA((planes,)),
+        ],
     )(haloed, both)
 
 
@@ -568,7 +631,7 @@
     devices = blocks_z * blocks_y
     place = planes * rows
     fits = place == LANES and 2 * count == LANES and half == 8 and blocks_z == 8
-    if not fits or count != CHUNKS * devices or replicas % 2 or rows % 8 or planes != 8 or devices % 8:
+    if not fits or count != CHUNKS * devices or replicas % 2 or rows != 16 or planes != 8 or devices % 8:
         return plain(charges, kernel)
     size = 2 * half
     per = LANES // size
@@ -578,10 +641,13 @@
         high, low = table(lines_x[chunk].reshape(devices // per, LANES, width))
         table_x.append(jnp.concatenate([high, low], axis=1).reshape(-1, width))
         table_f += table(refined(lines_x[chunk], 1).reshape(-1, 2 * width))
-    table_y = table(y_table(count, planes, rows))
-    tables = [*table_x, *table(line_table(count, devices)), *table_y, *z_tables(count, blocks_z), *table_f]
+    lines_y = y_table(count, planes, rows)
+    tables = [
+        *table(line_table(count, devices)), *table_x, *table(lines_y), *table(lines_y.T),
+        *z_tables(count, blocks_z), *table_f,
+    ]
+    arrays = [charges.reshape(place, width), kernel.reshape(place, count), *tables]
     deep = devices * size
-    vmem = pl.BlockSpec(memory_space=pltpu.VMEM)
     block = lambda *shape: pltpu.VMEM(shape, jnp.float32)
     dma = pltpu.SemaphoreType.DMA
     stage = [block(planes, deep), block(2 * planes, deep), block(4, 8, deep)]
@@ -591,12 +657,14 @@
     ]
     haloed = pl.pallas_call(
         functools.partial(main_kernel, (count, blocks_z, blocks_y, half, len(tables))),
-        out_shape=jax.ShapeDtypeStruct((planes + 3, rows + 8, 2 * width), jnp.float32),
-        in_specs=[vmem, vmem] + [pl.BlockSpec(memory_space=pl.ANY)] * len(tables),
-        out_specs=vmem,
+        out_shape=jax.ShapeDtypeStruct((planes + 3, 3 * rows, 2 * width), jnp.bfloat16),
+        in_specs=[pl.BlockSpec(memory_space=pl.ANY)] * len(arrays),
+        out_specs=pl.BlockSpec(memory_space=pl.ANY),
         scratch_shapes=[
-            *(pltpu.VMEM(t.shape, t.dtype) for t in tables),
-            dma((len(tables),)), dma((CHUNKS, 2, devices)), dma((CHUNKS, 2, devices)), dma((CHUNKS, 2, 8)),
+            *(pltpu.VMEM(a.shape, a.dtype) for a in arrays),
+            dma((len(arrays),)), dma((CHUNKS, 2)), dma((CHUNKS, 2)), dma((CHUNKS, 2)),
+            dma((4,)), block(planes + 3, rows + 8, 2 * width),
+            pltpu.VMEM((planes + 3, 3 * rows, 2 * width), jnp.bfloat16),
             block(devices * (size + 8), LANES), block(deep, LANES),
             block(devices * (size + 8), LANES), block(deep, LANES),
             block(deep, LANES), block(deep, LANES),
@@ -607,7 +675,7 @@
         compiler_params=pltpu.CompilerParams(
             collective_id=0, has_side_effects=True, vmem_limit_bytes=60 * 1024 * 1024
         ),
-    )(charges.reshape(place, width), kernel.reshape(place, count), *tables)
+    )(*arrays)
     return refine(haloed, planes, rows, 2 * width)
 
 

time: 55.2 us -> 45.7 us (0.83)
  Pallas kernels: 55 us -> 45.5 us
    pallas_call x1, Pallas kernels: 48.9 us -> 40.5 us  [per_device(): pl.pallas_call(functools.partial(main_kernel, (count, blocks_z, blocks_y,...]
    pallas_call x1, Pallas kernels: 6.17 us -> 5.02 us  [refine(): pl.pallas_call(refine_kernel, out_shape=jax.ShapeDtypeStruct(shape, jnp.f...]
where the time goes in v3:
time: 45.7 us; the launch traced here: 45.5 us
  Pallas kernels  45.5 us (100%)
    pallas_call x1, Pallas kernels, per_device(): pl.pallas_call(functools.partial(main_kernel, (count, blocks_z, blocks_y,...  40.5 us
    pallas_call x1, Pallas kernels, refine(): pl.pallas_call(refine_kernel, out_shape=jax.ShapeDtypeStruct(shape, jnp.f...  5.02 us

profile of v3, /device:TPU:0, one launch (start us, length us, event | category | flops | bytes accessed | tf_op | source)
XLA Modules:
  0.0 45.5 jit_solution(9419873345983247335)
XLA Ops:
  0.0 40.5 %shard_map.181.x_ref = bf16[11,48,2048]{2,1,0:T(8,128)(2,1)} custom-call(f32[128,1024]{1,0:T(8,128)} %bitcast.2, f32[128,64]{1,0:T(8,128)} %bitcast.3, bf16[256,64]{1,0:T(8,128)(2,1)} %constant.42.clone.refs_2_, bf16[256,64]{1,0:T(8,128)(2,1)} %constant.43.clone.refs_3_, bf16[1024,1024]{1,0:T(8,128)(2,1)} %constant.52.refs_4_, ...), custom_call_target="tpu_custom_call" | custom-call | tf_op jit(solution)/shard_map/pallas_call | solution.py:658
  40.5 5.0 %shard_map.182 = f32[16,32,2048]{2,1,0:T(8,128)} custom-call(bf16[11,48,2048]{2,1,0:T(8,128)(2,1)} %shard_map.181.x_ref, bf16[64,192]{1,0:T(8,128)(2,1)} %constant.50.clone.r_ref), custom_call_target="tpu_custom_call" | custom-call | tf_op jit(solution)/shard_map/pallas_call | solution.py:610

commit v4 on v3

--- a/solution.py
+++ b/solution.py
@@ -428,13 +428,13 @@
     devices = blocks_z * blocks_y
     planes = count // blocks_z
     sources = refs[: 2 + n_tables]
-    out = refs[2 + n_tables]
+    packed = refs[2 + n_tables]
     loaded = refs[3 + n_tables : 5 + 2 * n_tables]
     (q_ref, k_ref), tables = loaded[:2], loaded[2:]
     rest = list(refs[5 + 2 * n_tables :])
-    load_sem, sent_sem, back_sem, rim_sem, out_sem, total, packed = rest[:7]
-    sent, held, back, home, own = (rest[7 + 2 * i : 9 + 2 * i] for i in range(5))
-    stages, rims = (rest[17:20], rest[20:23]), (rest[23:28], rest[28:33])
+    load_sem, sent_sem, back_sem, rim_sem, total = rest[:5]
+    sent, held, back, home, own = (rest[5 + 2 * i : 7 + 2 * i] for i in range(5))
+    stages, rims = (rest[15:18], rest[18:21]), (rest[21:26], rest[26:31])
     table_k, table_x, table_y, table_b, table_z, table_f = (
         tables[0:2], tables[2:4], tables[4:6], tables[6:8], tables[8:10], tables[10:14]
     )
@@ -534,13 +534,6 @@
         packed[first:last, rows : 2 * rows, :] = low
 
     pack_own(1, planes + 1)
-    inside, around = (pl.ds(1, planes), pl.ds(0, 2 * rows)), (pl.ds(0, planes + 3), pl.ds(2 * rows, 16))
-    first, last = (pl.ds(0, 1), pl.ds(0, 2 * rows)), (pl.ds(planes + 1, 2), pl.ds(0, 2 * rows))
-    stores = [
-        pltpu.make_async_copy(packed.at[span], out.at[span], out_sem.at[i])
-        for i, span in enumerate((inside, around, first, last))
-    ]
-    stores[0].start()
     for chunk in range(CHUNKS):
         with scope(f"wait_rim{chunk}"):
             borders[chunk].wait_recv()
@@ -557,39 +550,31 @@
             sides = total[:, rows:, :] + sides
             high = sides.astype(jnp.bfloat16).astype(jnp.float32)
             packed[:, 2 * rows :, :] = jnp.concatenate([high, sides - high], axis=1).astype(jnp.bfloat16)
-            stores[1].start()
             for i, place in enumerate((0, planes + 1, planes + 2)):
                 high, low = split(total[place, :rows, :] + ends[i])
                 packed[place, :rows, :] = high
                 packed[place, rows : 2 * rows, :] = low
-    for store in stores[2:]:
-        store.start()
     with scope("wait_sends"):
         for copy in there + returns + borders:
             copy.wait_send()
+
+
+STEP = 2
+
+
+def refine_kernel(x_ref, r_ref, o_ref, made, out_sem):
+    planes = x_ref.shape[0] - 3
+    stores = []
+    for p in range(0, planes, STEP):
+        with jax.named_scope(f"refine{p}"):
+            near = x_ref[p : p + STEP + 3].reshape((STEP + 3) * x_ref.shape[1], x_ref.shape[2])
+            span = pl.ds(2 * p, 2 * STEP)
+            made[span] = mul(r_ref[...], near).reshape(2 * STEP, -1, made.shape[2])
+            stores.append(pltpu.make_async_copy(made.at[span], o_ref.at[span], out_sem.at[p // STEP]))
+            stores[-1].start()
+    with jax.named_scope("refine_store"):
         for store in stores:
             store.wait()
-
-
-def refine_kernel(x_ref, r_ref, o_ref, held, made, sem, out_sem):
-    planes = x_ref.shape[0] - 3
-    loads = [
-        pltpu.make_async_copy(x_ref.at[p], held.at[p], sem.at[p]) for p in range(planes + 3)
-    ]
-    for load in loads:
-        load.start()
-    for load in loads[:3]:
-        load.wait()
-    stores = []
-    for p in range(planes):
-        loads[p + 3].wait()
-        near = held[p : p + 4].reshape(4 * held.shape[1], held.shape[2])
-        made[2 * p : 2 * p + 2] = mul(r_ref[...], near).reshape(2, -1, made.shape[2])
-        span = pl.ds(2 * p, 2)
-        stores.append(pltpu.make_async_copy(made.at[span], o_ref.at[span], out_sem.at[p]))
-        stores[-1].start()
-    for store in stores:
-        store.wait()
 
 
 def rim_table(count):
@@ -605,20 +590,20 @@
     middle = along_y[:, 1 : rows + 1]
     sides = np.concatenate([along_y[:, :1], along_y[:, rows + 1 :], np.zeros((2 * rows, 5))], axis=1)
     along_y = np.concatenate([middle, middle, sides, sides], axis=1)
-    both = jnp.asarray(np.kron(rim_table(1), along_y), jnp.bfloat16)
+    both = jnp.asarray(np.kron(rim_table(STEP), along_y), jnp.bfloat16)
     shape = (2 * planes, 2 * rows, width)
     return pl.pallas_call(
         refine_kernel,
         out_shape=jax.ShapeDtypeStruct(shape, jnp.float32),
         in_specs=[
-            pl.BlockSpec(memory_space=pl.ANY),
+            pl.BlockSpec(memory_space=pltpu.VMEM),
             pl.BlockSpec(memory_space=pltpu.VMEM),
         ],
         out_specs=pl.BlockSpec(memory_space=pl.ANY),
         scratch_shapes=[
-            pltpu.VMEM(haloed.shape, haloed.dtype), pltpu.VMEM(shape, jnp.float32),
-            pltpu.SemaphoreType.DMA((planes + 3,)), pltpu.SemaphoreType.DMA((planes,)),
+            pltpu.VMEM(shape, jnp.float32), pltpu.SemaphoreType.DMA((planes // STEP,)),
         ],
+        compiler_params=pltpu.CompilerParams(vmem_limit_bytes=16 * 1024 * 1024),
     )(haloed, both)
 
 
@@ -657,14 +642,13 @@
     ]
     haloed = pl.pallas_call(
         functools.partial(main_kernel, (count, blocks_z, blocks_y, half, len(tables))),
-        out_shape=jax.ShapeDtypeStruct((planes + 3, 3 * rows, 2 * width), jnp.bfloat16),
+        out_shape=pltpu.VMEM((planes + 3, 3 * rows, 2 * width), jnp.bfloat16),
         in_specs=[pl.BlockSpec(memory_space=pl.ANY)] * len(arrays),
-        out_specs=pl.BlockSpec(memory_space=pl.ANY),
+        out_specs=pl.BlockSpec(memory_space=pltpu.VMEM),
         scratch_shapes=[
             *(pltpu.VMEM(a.shape, a.dtype) for a in arrays),
             dma((len(arrays),)), dma((CHUNKS, 2)), dma((CHUNKS, 2)), dma((CHUNKS, 2)),
-            dma((4,)), block(planes + 3, rows + 8, 2 * width),
-            pltpu.VMEM((planes + 3, 3 * rows, 2 * width), jnp.bfloat16),
+            block(planes + 3, rows + 8, 2 * width),
             block(devices * (size + 8), LANES), block(deep, LANES),
             block(devices * (size + 8), LANES), block(deep, LANES),
             block(deep, LANES), block(deep, LANES),

time: 45.7 us -> 42 us (0.919)
  Pallas kernels: 45.5 us -> 41.8 us
    pallas_call x1, Pallas kernels: 5.02 us -> 2.35 us  [refine(): pl.pallas_call(refine_kernel, out_shape=jax.ShapeDtypeStruct(shape, jnp.f...]
    pallas_call x1, Pallas kernels: 40.5 us -> 39.4 us  [per_device(): pl.pallas_call(functools.partial(main_kernel, (count, blocks_z, blocks_y,...]
where the time goes in v4:
time: 42 us; the launch traced here: 41.8 us
  Pallas kernels  41.8 us (100%)
    pallas_call x1, Pallas kernels, per_device(): pl.pallas_call(functools.partial(main_kernel, (count, blocks_z, blocks_y,...  39.4 us
    pallas_call x1, Pallas kernels, refine(): pl.pallas_call(refine_kernel, out_shape=jax.ShapeDtypeStruct(shape, jnp.f...  2.35 us

profile of v4, /device:TPU:0, one launch (start us, length us, event | category | flops | bytes accessed | tf_op | source)
XLA Modules:
  0.0 41.8 jit_solution(3388915445530781206)
XLA Ops:
  0.0 0.0 copy-start
  0.0 39.4 %shard_map.181.x_ref = bf16[11,48,2048]{2,1,0:T(8,128)(2,1)S(1)} custom-call(f32[128,1024]{1,0:T(8,128)} %bitcast.2, f32[128,64]{1,0:T(8,128)} %bitcast.3, bf16[256,64]{1,0:T(8,128)(2,1)} %constant.42.clone.refs_2_, bf16[256,64]{1,0:T(8,128)(2,1)} %constant.43.clone.refs_3_, bf16[1024,1024]{1,0:T(8,128)(2,1)} %constant.52.refs_4_, ...), custom_call_target="tpu_custom_call" | custom-call | tf_op jit(solution)/shard_map/pallas_call | solution.py:643
  39.4 0.0 copy-done
  39.5 2.4 %shard_map.182 = f32[16,32,2048]{2,1,0:T(8,128)} custom-call(bf16[11,48,2048]{2,1,0:T(8,128)(2,1)S(1)} %shard_map.181.x_ref, bf16[128,240]{1,0:T(8,128)(2,1)S(1)} %copy-done), custom_call_target="tpu_custom_call" | custom-call | tf_op jit(solution)/shard_map/pallas_call | solution.py:595
Async XLA Ops:
  0.0 39.5 %copy-start = (bf16[128,240]{1,0:T(8,128)(2,1)S(1)}, bf16[128,240]{1,0:T(8,128)(2,1)}, u32[]{:S(2)}) copy-start(bf16[128,240]{1,0:T(8,128)(2,1)} %constant.50.clone.r_ref) | copy-start | bytes 184324

commit v5 on v4

--- a/solution.py
+++ b/solution.py
@@ -234,12 +234,12 @@
 
 def remote(source, target, sems, place):
     return pltpu.make_async_remote_copy(
-        src_ref=source, dst_ref=target, send_sem=sems.at[0], recv_sem=sems.at[1],
+        src_ref=source, dst_ref=target, send_sem=sems[0], recv_sem=sems[1],
         device_id=place, device_id_type=MESH,
     )
 
 
-def exchange(blocks_z, blocks_y, rows, source, target, sems):
+def exchange(blocks_z, blocks_y, rows, source, target, sems, halves=False):
     size = blocks_z * blocks_y // GROUPS
     devices = size * GROUPS
     me = lax.axis_index("gz") * blocks_y + lax.axis_index("gy")
@@ -255,7 +255,8 @@
             there = remote(
                 source.at[pl.ds(pl.multiple_of(other * pitch_from, 8), rows)],
                 target.at[pl.ds(pl.multiple_of(me * pitch_to, 8), rows)],
-                sems, (other // blocks_y, lax.rem(other, blocks_y)),
+                (sems.at[0], sems.at[1 + lax.rem(flip_high + turn, 2) if halves else 1]),
+                (other // blocks_y, lax.rem(other, blocks_y)),
             )
             if step == 0 and flip_high == flip_low:
                 pl.when(other != me)(there.start)
@@ -265,10 +266,16 @@
     mine_from = pl.ds(pl.multiple_of(me * pitch_from, 8), span)
     target[pl.ds(pl.multiple_of(me * pitch_to, 8), span), :] = source[mine_from, :]
     other = lax.rem(me + 1, devices)
-    count = pl.ds(0, (devices - 1) * rows)
-    return remote(
-        source.at[count], target.at[count], sems, (other // blocks_y, lax.rem(other, blocks_y))
-    )
+
+    def counter(number, senders):
+        span = pl.ds(0, senders * rows)
+        place = (other // blocks_y, lax.rem(other, blocks_y))
+        return remote(source.at[span], target.at[span], (sems.at[0], sems.at[number]), place)
+
+    everything = counter(1, devices - 1)
+    if halves:
+        return everything, counter(1, devices // 2 - 1), counter(2, devices // 2)
+    return everything, everything
 
 
 def swap_parts(values):
@@ -409,18 +416,15 @@
     return remote(sizes[0].at[count], sizes[1].at[count], sems, (next_z, gy))
 
 
-def rim_lines(planes, rims):
+def rim_lines(rims):
     low_z, high_z, low_y, high_y, corner = rims
+    planes = low_y.shape[0]
     empty = jnp.zeros((5, low_z.shape[1]), jnp.float32)
-    tiles = [corner[0, 0:1, :], corner[1, 0:2, :], empty]
-    for p in range(planes):
-        tiles += [
-            low_y[p : p + 1, :], high_y[p : p + 1, :], high_y[planes + p : planes + p + 1, :], empty,
-        ]
-    tiles += [corner[2, 0:1, :], corner[3, 0:2, :], empty]
-    tiles += [corner[2, 1:2, :], corner[3, 2:4, :], empty]
-    tiles += [jnp.zeros((8, low_z.shape[1]), jnp.float32)]
-    return jnp.concatenate([low_z[...], high_z[...], *tiles], axis=0)
+    tiles = [low_z[...], high_z[...]]
+    tiles += [low_y[...], corner[0, 0:1, :], corner[2, 0:2, :], empty]
+    tiles += [high_y[:planes, :], corner[1, 0:1, :], corner[3, 0:1, :], corner[3, 2:3, :], empty]
+    tiles += [high_y[planes:, :], corner[1, 1:2, :], corner[3, 1:2, :], corner[3, 3:4, :], empty]
+    return jnp.concatenate(tiles, axis=0)
 
 
 def main_kernel(sizes, *refs):
@@ -432,9 +436,11 @@
     loaded = refs[3 + n_tables : 5 + 2 * n_tables]
     (q_ref, k_ref), tables = loaded[:2], loaded[2:]
     rest = list(refs[5 + 2 * n_tables :])
-    load_sem, sent_sem, back_sem, rim_sem, total = rest[:5]
-    sent, held, back, home, own = (rest[5 + 2 * i : 7 + 2 * i] for i in range(5))
-    stages, rims = (rest[15:18], rest[18:21]), (rest[21:26], rest[26:31])
+    load_sem, sent_sem, back_sem, rim_sem, total, edge = rest[:6]
+    sent, held, back, home = (rest[6 + 2 * i : 8 + 2 * i] for i in range(4))
+    own = rest[14:17]
+    stages = [rest[17 + 3 * i : 20 + 3 * i] for i in range(3)]
+    rims = [rest[26 + 5 * i : 31 + 5 * i] for i in range(2)]
     table_k, table_x, table_y, table_b, table_z, table_f = (
         tables[0:2], tables[2:4], tables[4:6], tables[6:8], tables[8:10], tables[10:14]
     )
@@ -492,7 +498,7 @@
     with scope("wait_there0"):
         for load in loads[6:12]:
             load.wait()
-        there[0].wait_recv()
+        there[0][1].wait_recv()
     y_pairs = ((table_y[0][...], table_y[1][...]), (table_b[0][...], table_b[1][...]))
     z_pair = (table_z[0][...], table_z[1][...])
     shape = (count, blocks_z, blocks_y, half)
@@ -501,75 +507,86 @@
     with scope("return0"):
         returns = [exchange(blocks_z, blocks_y, size, back[0], home[0], back_sem.at[0])]
     with scope("wait_there1"):
-        there[1].wait_recv()
+        there[1][1].wait_recv()
     with scope("middle1"):
         middle_stage(shape, held[1], *y_pairs, *z_pair, green[:, LANES:], back[1])
     with scope("return1"):
-        returns.append(exchange(blocks_z, blocks_y, size, back[1], home[1], back_sem.at[1]))
+        returns.append(exchange(blocks_z, blocks_y, size, back[1], home[1], back_sem.at[1], True))
     for load in loads[12:]:
         load.wait()
+    deep = home[0].shape[0]
+    near = pl.multiple_of(me // (devices // 2) * (deep // 2), LANES)
+    far = pl.multiple_of(deep // 2 - near, LANES)
+    pieces = (
+        (0, pl.ds(0, deep), returns[0][1]), (1, pl.ds(near, deep // 2), returns[1][1]),
+        (1, pl.ds(far, deep // 2), returns[1][2]),
+    )
     borders = []
-    fine = [(table_f[2 * c][...], table_f[2 * c + 1][...]) for c in range(CHUNKS)]
-    for chunk in range(CHUNKS):
-        with scope(f"wait_back{chunk}"):
-            returns[chunk].wait_recv()
-        with scope(f"turn{chunk}"):
-            turned = jnp.transpose(home[chunk][...])
-            own[chunk][...] = turned
-        with scope(f"send_rim{chunk}"):
+
+    def fine_of(number):
+        chunk, span, _ = pieces[number]
+        return table_f[2 * chunk][span, :], table_f[2 * chunk + 1][span, :]
+
+    half_of = me // (devices // 2)
+    slots = (rims[0], *([r.at[s] for r in rims[1]] for s in (half_of, 1 - half_of)))
+    rim_sems = [
+        (rim_sem.at[0, 0], rim_sem.at[1, 0]),
+        (rim_sem.at[0, 1], rim_sem.at[1, 1 + half_of]),
+        (rim_sem.at[0, 2], rim_sem.at[1, 2 - half_of]),
+    ]
+    for number, (chunk, span, coming) in enumerate(pieces):
+        with scope(f"wait_back{number}"):
+            coming.wait_recv()
+        with scope(f"turn{number}"):
+            turned = jnp.transpose(home[chunk][span, :])
+            own[number][...] = turned
+        with scope(f"send_rim{number}"):
             borders.append(send_rims(
-                blocks_z, blocks_y, planes, rows, own[chunk], home, stages[chunk], rims[chunk], rim_sem.at[chunk]
+                blocks_z, blocks_y, planes, rows, own[number], home, stages[number], slots[number],
+                rim_sems[number],
             ))
-        with scope(f"own{chunk}"):
-            made = mul3_rows(split(turned), fine[chunk]).reshape(planes, rows, -1)
-            if chunk:
-                made = total[1 : planes + 1, :rows, :] + made
-            total[1 : planes + 1, :rows, :] = made
+        with scope(f"own{number}"):
+            made = mul3_rows(split(turned), fine_of(number))
+            total[...] = total[...] + made if number else made
     flat = 3 * rows
 
-    def pack_own(first, last):
-        values = total[first:last, :rows, :]
+    def pack(place, values):
         high, low = split(values)
-        packed[first:last, :rows, :] = high
-        packed[first:last, rows : 2 * rows, :] = low
-
-    pack_own(1, planes + 1)
-    for chunk in range(CHUNKS):
-        with scope(f"wait_rim{chunk}"):
-            borders[chunk].wait_recv()
-        with scope(f"rim{chunk}"):
-            made = mul3_rows(split(rim_lines(planes, rims[chunk])), fine[chunk])
-            sides = 8 * (planes + 3)
-            ends = made[:flat].reshape(3, rows, -1)
-            sides = made[flat : flat + sides].reshape(planes + 3, 8, -1)
-            if not chunk:
-                total[:, rows:, :] = sides
-                total[0:1, :rows, :] = ends[0:1]
-                total[planes + 1 :, :rows, :] = ends[1:]
+        packed[place, :] = high
+        packed[pl.ds(place.start + place.size, place.size), :] = low
+
+    for p in range(planes):
+        pack(pl.ds(2 * (p + 1) * rows, rows), total[p * rows : (p + 1) * rows, :])
+    for number in range(len(pieces)):
+        with scope(f"wait_rim{number}"):
+            borders[number].wait_recv()
+        with scope(f"rim{number}"):
+            made = mul3_rows(split(rim_lines(slots[number])), fine_of(number))
+            if number:
+                made = edge[...] + made
+            if number < len(pieces) - 1:
+                edge[...] = made
                 continue
-            sides = total[:, rows:, :] + sides
-            high = sides.astype(jnp.bfloat16).astype(jnp.float32)
-            packed[:, 2 * rows :, :] = jnp.concatenate([high, sides - high], axis=1).astype(jnp.bfloat16)
-            for i, place in enumerate((0, planes + 1, planes + 2)):
-                high, low = split(total[place, :rows, :] + ends[i])
-                packed[place, :rows, :] = high
-                packed[place, rows : 2 * rows, :] = low
+            for i, p in enumerate((0, planes + 1, planes + 2)):
+                pack(pl.ds(2 * p * rows, rows), made[i * rows : (i + 1) * rows, :])
+            pack(pl.ds(2 * (planes + 3) * rows, flat), made[flat:, :])
     with scope("wait_sends"):
-        for copy in there + returns + borders:
+        for copy in [there[0][0], there[1][0], returns[0][0], returns[1][0], *borders]:
             copy.wait_send()
 
 
 STEP = 2
 
 
-def refine_kernel(x_ref, r_ref, o_ref, made, out_sem):
-    planes = x_ref.shape[0] - 3
+def refine_kernel(rows, x_ref, r_ref, o_ref, made, out_sem):
+    planes = made.shape[0] // 2
     stores = []
     for p in range(0, planes, STEP):
         with jax.named_scope(f"refine{p}"):
-            near = x_ref[p : p + STEP + 3].reshape((STEP + 3) * x_ref.shape[1], x_ref.shape[2])
+            near = x_ref[2 * p * rows : 2 * (p + STEP + 3) * rows, :]
+            near = jnp.concatenate([near, x_ref[2 * (planes + 3) * rows :, :]], axis=0)
             span = pl.ds(2 * p, 2 * STEP)
-            made[span] = mul(r_ref[...], near).reshape(2 * STEP, -1, made.shape[2])
+            made[span] = mul(r_ref[p // STEP], near).reshape(2 * STEP, -1, made.shape[2])
             stores.append(pltpu.make_async_copy(made.at[span], o_ref.at[span], out_sem.at[p // STEP]))
             stores[-1].start()
     with jax.named_scope("refine_store"):
@@ -585,15 +602,27 @@
     return made
 
 
+def refine_tables(planes, rows):
+    along_y = rim_table(rows)
+    along_z = rim_table(planes)
+    middle, sides = along_y[:, 1 : rows + 1], np.delete(along_y, np.arange(1, rows + 1), axis=1)
+    order = [*range(1, planes + 1), 0, planes + 1, planes + 2]
+    made = []
+    for p in range(0, planes, STEP):
+        lines = along_z[2 * p : 2 * (p + STEP)]
+        own = np.kron(lines[:, p : p + STEP + 3], np.concatenate([middle, middle], axis=1))
+        beside = np.einsum("ze,ys->zyse", lines[:, order], sides)
+        beside = np.pad(beside, ((0, 0), (0, 0), (0, 0), (0, rows - len(order))))
+        beside = beside.reshape(own.shape[0], 3 * rows)
+        made.append(np.concatenate([own, beside, beside], axis=1))
+    return np.stack(made)
+
+
 def refine(haloed, planes, rows, width):
-    along_y = rim_table(rows)
-    middle = along_y[:, 1 : rows + 1]
-    sides = np.concatenate([along_y[:, :1], along_y[:, rows + 1 :], np.zeros((2 * rows, 5))], axis=1)
-    along_y = np.concatenate([middle, middle, sides, sides], axis=1)
-    both = jnp.asarray(np.kron(rim_table(STEP), along_y), jnp.bfloat16)
+    tables = jnp.asarray(refine_tables(planes, rows), jnp.bfloat16)
     shape = (2 * planes, 2 * rows, width)
     return pl.pallas_call(
-        refine_kernel,
+        functools.partial(refine_kernel, rows),
         out_shape=jax.ShapeDtypeStruct(shape, jnp.float32),
         in_specs=[
             pl.BlockSpec(memory_space=pltpu.VMEM),
@@ -604,7 +633,7 @@
             pltpu.VMEM(shape, jnp.float32), pltpu.SemaphoreType.DMA((planes // STEP,)),
         ],
         compiler_params=pltpu.CompilerParams(vmem_limit_bytes=16 * 1024 * 1024),
-    )(haloed, both)
+    )(haloed, tables)
 
 
 def per_device(charges, kernel):
@@ -635,26 +664,27 @@
     deep = devices * size
     block = lambda *shape: pltpu.VMEM(shape, jnp.float32)
     dma = pltpu.SemaphoreType.DMA
-    stage = [block(planes, deep), block(2 * planes, deep), block(4, 8, deep)]
-    rim = [
-        block(rows, deep), block(2 * rows, deep), block(planes, deep), block(2 * planes, deep),
-        block(4, 8, deep),
+    widths = (deep, deep // 2, deep // 2)
+    stages = [block(*shape) for w in widths for shape in ((planes, w), (2 * planes, w), (4, 8, w))]
+    rims = [
+        block(*lead, *shape, w)
+        for lead, w in (((), deep), ((2,), deep // 2))
+        for shape in ((rows,), (2 * rows,), (planes,), (2 * planes,), (4, 8))
     ]
     haloed = pl.pallas_call(
         functools.partial(main_kernel, (count, blocks_z, blocks_y, half, len(tables))),
-        out_shape=pltpu.VMEM((planes + 3, 3 * rows, 2 * width), jnp.bfloat16),
+        out_shape=pltpu.VMEM((2 * (planes + 6) * rows, 2 * width), jnp.bfloat16),
         in_specs=[pl.BlockSpec(memory_space=pl.ANY)] * len(arrays),
         out_specs=pl.BlockSpec(memory_space=pltpu.VMEM),
         scratch_shapes=[
             *(pltpu.VMEM(a.shape, a.dtype) for a in arrays),
-            dma((len(arrays),)), dma((CHUNKS, 2)), dma((CHUNKS, 2)), dma((CHUNKS, 2)),
-            block(planes + 3, rows + 8, 2 * width),
+            dma((len(arrays),)), dma((CHUNKS, 2)), dma((CHUNKS, 3)), dma((2, 3)),
+            block(place, 2 * width), block(6 * rows, 2 * width),
             block(devices * (size + 8), LANES), block(deep, LANES),
             block(devices * (size + 8), LANES), block(deep, LANES),
             block(deep, LANES), block(deep, LANES),
             block(deep, LANES), block(deep, LANES),
-            block(place, deep), block(place, deep),
-            *stage, *stage, *rim, *rim,
+            *(block(place, w) for w in widths), *stages, *rims,
         ],
         compiler_params=pltpu.CompilerParams(
             collective_id=0, has_side_effects=True, vmem_limit_bytes=60 * 1024 * 1024

time: 42 us -> 41.2 us (0.981)
  Pallas kernels: 41.8 us -> 41 us
    pallas_call x1, Pallas kernels: 39.4 us -> 38.6 us  [per_device(): pl.pallas_call(functools.partial(main_kernel, (count, blocks_z, blocks_y,...]
where the time goes in v5:
time: 41.2 us; the launch traced here: 41 us
  Pallas kernels  41 us (100%)
    pallas_call x1, Pallas kernels, per_device(): pl.pallas_call(functools.partial(main_kernel, (count, blocks_z, blocks_y,...  38.6 us
    pallas_call x1, Pallas kernels, refine(): pl.pallas_call(functools.partial(refine_kernel, rows), out_shape=jax.Shap...  2.36 us

profile of v5, /device:TPU:0, one launch (start us, length us, event | category | flops | bytes accessed | tf_op | source)
XLA Modules:
  0.0 41.0 jit_solution(831400912678537523)
XLA Ops:
  0.0 0.0 copy-start
  0.0 38.6 %shard_map.181.x_ref = bf16[448,2048]{1,0:T(8,128)(2,1)S(1)} custom-call(f32[128,1024]{1,0:T(8,128)} %bitcast.2, f32[128,64]{1,0:T(8,128)} %bitcast.3, bf16[256,64]{1,0:T(8,128)(2,1)} %constant.42.clone.refs_2_, bf16[256,64]{1,0:T(8,128)(2,1)} %constant.43.clone.refs_3_, bf16[1024,1024]{1,0:T(8,128)(2,1)} %constant.52.refs_4_, ...), custom_call_target="tpu_custom_call" | custom-call | tf_op jit(solution)/shard_map/pallas_call | solution.py:674
  38.6 0.0 copy-done
  38.7 2.4 %shard_map.182 = f32[16,32,2048]{2,1,0:T(8,128)} custom-call(bf16[448,2048]{1,0:T(8,128)(2,1)S(1)} %shard_map.181.x_ref, bf16[4,128,256]{2,1,0:T(8,128)(2,1)S(1)} %copy-done), custom_call_target="tpu_custom_call" | custom-call | tf_op jit(solution)/shard_map/pallas_call | solution.py:624
Async XLA Ops:
  0.0 38.6 %copy-start = (bf16[4,128,256]{2,1,0:T(8,128)(2,1)S(1)}, bf16[4,128,256]{2,1,0:T(8,128)(2,1)}, u32[]{:S(2)}) copy-start(bf16[4,128,256]{2,1,0:T(8,128)(2,1)} %constant.50.clone.r_ref) | copy-start | bytes 786436

commit v6 on v5

--- a/solution.py
+++ b/solution.py
@@ -248,17 +248,21 @@
     turn = lax.rem(high + low, 2)
     pitch_from, pitch_to = source.shape[0] // devices, target.shape[0] // devices
 
-    for flip_high, flip_low in ((1, 0), (1, 1), (0, 1), (0, 0)):
-        far = lax.rem(high + flip_high + turn, 2) * 2 + lax.rem(low + flip_low + turn, 2)
+    order = [(flip + turn, low + other + turn, flip == other) for flip, other in ((1, 0), (1, 1), (0, 1), (0, 0))]
+    if halves:
+        order = [(1, 1 - high, False), (0, high, True), (1, high, False), (0, 1 - high, True)]
+    for flip, other_low, own in order:
+        across = lax.rem(high + flip, 2)
+        far = across * 2 + lax.rem(other_low, 2)
         for step in range(size):
             other = far * size + lax.rem(inner + step, size)
             there = remote(
                 source.at[pl.ds(pl.multiple_of(other * pitch_from, 8), rows)],
                 target.at[pl.ds(pl.multiple_of(me * pitch_to, 8), rows)],
-                (sems.at[0], sems.at[1 + lax.rem(flip_high + turn, 2) if halves else 1]),
+                (sems.at[0], sems.at[1 + flip if halves else 1]),
                 (other // blocks_y, lax.rem(other, blocks_y)),
             )
-            if step == 0 and flip_high == flip_low:
+            if step == 0 and own:
                 pl.when(other != me)(there.start)
             else:
                 there.start()
@@ -557,11 +561,24 @@
 
     for p in range(planes):
         pack(pl.ds(2 * (p + 1) * rows, rows), total[p * rows : (p + 1) * rows, :])
-    for number in range(len(pieces)):
+    turn = lax.rem(lax.rem(me // blocks_y, blocks_z // 2), blocks_z // 2 - 1)
+    border = jnp.where(turn == 0, 1, 0)
+    late = lax.rem(half_of + 1 + border, 2)
+    rim_order = [(0, pl.ds(0, deep), rims[0], rim_sem.at[1, 0])]
+    for slot in (1 - late, late):
+        span = pl.ds(pl.multiple_of(slot * (deep // 2), LANES), deep // 2)
+        rim_order.append((1, span, [r.at[slot] for r in rims[1]], rim_sem.at[1, 1 + slot]))
+    for number, (chunk, span, slot, sem) in enumerate(rim_order):
         with scope(f"wait_rim{number}"):
-            borders[number].wait_recv()
+            count = pl.ds(0, 3 * (planes + rows + 3) * own[number].shape[1] // LANES)
+            other = lax.rem(me + 1, devices)
+            remote(
+                home[0].at[count], home[1].at[count], (rim_sem.at[0, number], sem),
+                (other // blocks_y, lax.rem(other, blocks_y)),
+            ).wait_recv()
         with scope(f"rim{number}"):
-            made = mul3_rows(split(rim_lines(slots[number])), fine_of(number))
+            fine = (table_f[2 * chunk][span, :], table_f[2 * chunk + 1][span, :])
+            made = mul3_rows(split(rim_lines(slot)), fine)
             if number:
                 made = edge[...] + made
             if number < len(pieces) - 1:

time: 41.2 us -> 40.9 us (level)
  no operation moved by 1% of the time
where the time goes in v6:
time: 40.9 us; the launch traced here: 40.8 us
  Pallas kernels  40.7 us (100%)
    pallas_call x1, Pallas kernels, per_device(): pl.pallas_call(functools.partial(main_kernel, (count, blocks_z, blocks_y,...  38.4 us
    pallas_call x1, Pallas kernels, refine(): pl.pallas_call(functools.partial(refine_kernel, rows), out_shape=jax.Shap...  2.36 us

profile of v6, /device:TPU:0, one launch (start us, length us, event | category | flops | bytes accessed | tf_op | source)
XLA Modules:
  0.0 40.8 jit_solution(17160855489895494347)
XLA Ops:
  0.0 0.0 copy-start
  0.0 38.4 %shard_map.181.x_ref = bf16[448,2048]{1,0:T(8,128)(2,1)S(1)} custom-call(f32[128,1024]{1,0:T(8,128)} %bitcast.2, f32[128,64]{1,0:T(8,128)} %bitcast.3, bf16[256,64]{1,0:T(8,128)(2,1)} %constant.42.clone.refs_2_, bf16[256,64]{1,0:T(8,128)(2,1)} %constant.43.clone.refs_3_, bf16[1024,1024]{1,0:T(8,128)(2,1)} %constant.52.refs_4_, ...), custom_call_target="tpu_custom_call" | custom-call | tf_op jit(solution)/shard_map/pallas_call | solution.py:691
  38.4 0.0 copy-done
  38.4 2.4 %shard_map.182 = f32[16,32,2048]{2,1,0:T(8,128)} custom-call(bf16[448,2048]{1,0:T(8,128)(2,1)S(1)} %shard_map.181.x_ref, bf16[4,128,256]{2,1,0:T(8,128)(2,1)S(1)} %copy-done), custom_call_target="tpu_custom_call" | custom-call | tf_op jit(solution)/shard_map/pallas_call | solution.py:641
Async XLA Ops:
  0.0 38.4 %copy-start = (bf16[4,128,256]{2,1,0:T(8,128)(2,1)S(1)}, bf16[4,128,256]{2,1,0:T(8,128)(2,1)}, u32[]{:S(2)}) copy-start(bf16[4,128,256]{2,1,0:T(8,128)(2,1)} %constant.50.clone.r_ref) | copy-start | bytes 786436

commit v7 on v6

--- a/solution.py
+++ b/solution.py
@@ -239,7 +239,7 @@
     )
 
 
-def exchange(blocks_z, blocks_y, rows, source, target, sems, halves=False):
+def exchange(blocks_z, blocks_y, rows, source, target, sems, form, halves=False):
     size = blocks_z * blocks_y // GROUPS
     devices = size * GROUPS
     me = lax.axis_index("gz") * blocks_y + lax.axis_index("gy")
@@ -249,8 +249,11 @@
     pitch_from, pitch_to = source.shape[0] // devices, target.shape[0] // devices
 
     order = [(flip + turn, low + other + turn, flip == other) for flip, other in ((1, 0), (1, 1), (0, 1), (0, 0))]
-    if halves:
-        order = [(1, 1 - high, False), (0, high, True), (1, high, False), (0, 1 - high, True)]
+    ends_first = [(1, 1 - high, False), (0, high, True), (1, high, False), (0, 1 - high, True)]
+    if form == 1:
+        order = ends_first
+    elif form == 2:
+        order = ends_first[2:] + ends_first[:2]
     for flip, other_low, own in order:
         across = lax.rem(high + flip, 2)
         far = across * 2 + lax.rem(other_low, 2)
@@ -493,12 +496,12 @@
     with scope("barrier"):
         pl.semaphore_wait(barrier, devices - 1)
     with scope("send0"):
-        there = [exchange(blocks_z, blocks_y, size + 2, sent[0], held[0], sent_sem.at[0])]
+        there = [exchange(blocks_z, blocks_y, size + 2, sent[0], held[0], sent_sem.at[0], 2)]
     with scope("x_lines1"):
         loads[5].wait()
         x_lines(1, charges)
     with scope("send1"):
-        there.append(exchange(blocks_z, blocks_y, size, sent[1], held[1], sent_sem.at[1]))
+        there.append(exchange(blocks_z, blocks_y, size, sent[1], held[1], sent_sem.at[1], 2))
     with scope("wait_there0"):
         for load in loads[6:12]:
             load.wait()
@@ -509,13 +512,13 @@
     with scope("middle0"):
         green = middle_stage(shape, held[0], *y_pairs, *z_pair, None, back[0])
     with scope("return0"):
-        returns = [exchange(blocks_z, blocks_y, size, back[0], home[0], back_sem.at[0])]
+        returns = [exchange(blocks_z, blocks_y, size, back[0], home[0], back_sem.at[0], 1)]
     with scope("wait_there1"):
         there[1][1].wait_recv()
     with scope("middle1"):
         middle_stage(shape, held[1], *y_pairs, *z_pair, green[:, LANES:], back[1])
     with scope("return1"):
-        returns.append(exchange(blocks_z, blocks_y, size, back[1], home[1], back_sem.at[1], True))
+        returns.append(exchange(blocks_z, blocks_y, size, back[1], home[1], back_sem.at[1], 1, True))
     for load in loads[12:]:
         load.wait()
     deep = home[0].shape[0]
@@ -597,15 +600,21 @@
 
 def refine_kernel(rows, x_ref, r_ref, o_ref, made, out_sem):
     planes = made.shape[0] // 2
+    width = made.shape[2] // 2
     stores = []
     for p in range(0, planes, STEP):
-        with jax.named_scope(f"refine{p}"):
-            near = x_ref[2 * p * rows : 2 * (p + STEP + 3) * rows, :]
-            near = jnp.concatenate([near, x_ref[2 * (planes + 3) * rows :, :]], axis=0)
-            span = pl.ds(2 * p, 2 * STEP)
-            made[span] = mul(r_ref[p // STEP], near).reshape(2 * STEP, -1, made.shape[2])
-            stores.append(pltpu.make_async_copy(made.at[span], o_ref.at[span], out_sem.at[p // STEP]))
-            stores[-1].start()
+        for half in range(2):
+            with jax.named_scope(f"refine{p}"):
+                lanes = pl.ds(half * width, width)
+                near = x_ref[pl.ds(2 * p * rows, 2 * (STEP + 3) * rows), lanes]
+                beside = x_ref[pl.ds(2 * (planes + 3) * rows, 6 * rows), lanes]
+                fine = mul(r_ref[p // STEP], jnp.concatenate([near, beside], axis=0))
+                place = (pl.ds(2 * p, 2 * STEP), slice(None), lanes)
+                made[place] = fine.reshape(2 * STEP, -1, width)
+                stores.append(
+                    pltpu.make_async_copy(made.at[place], o_ref.at[place], out_sem.at[len(stores)])
+                )
+                stores[-1].start()
     with jax.named_scope("refine_store"):
         for store in stores:
             store.wait()
@@ -647,7 +656,7 @@
         ],
         out_specs=pl.BlockSpec(memory_space=pl.ANY),
         scratch_shapes=[
-            pltpu.VMEM(shape, jnp.float32), pltpu.SemaphoreType.DMA((planes // STEP,)),
+            pltpu.VMEM(shape, jnp.float32), pltpu.SemaphoreType.DMA((2 * planes // STEP,)),
         ],
         compiler_params=pltpu.CompilerParams(vmem_limit_bytes=16 * 1024 * 1024),
     )(haloed, tables)

time: 40.9 us -> 39.1 us (0.956)
  the two profiles are of different devices: /device:TPU:0 before, /device:TPU:5 now
where the time goes in v7:
time: 39.1 us; the launch traced here: 39 us
  Pallas kernels  39 us (100%)
    pallas_call x1, Pallas kernels, per_device(): pl.pallas_call(functools.partial(main_kernel, (count, blocks_z, blocks_y,...  36.6 us
    pallas_call x1, Pallas kernels, refine(): pl.pallas_call(functools.partial(refine_kernel, rows), out_shape=jax.Shap...  2.31 us

profile of v7, /device:TPU:5, one launch (start us, length us, event | category | flops | bytes accessed | tf_op | source)
XLA Modules:
  0.0 39.0 jit_solution(6414232305562391554)
XLA Ops:
  0.0 0.0 copy-start
  0.0 36.6 %shard_map.181.x_ref = bf16[448,2048]{1,0:T(8,128)(2,1)S(1)} custom-call(f32[128,1024]{1,0:T(8,128)} %bitcast.2, f32[128,64]{1,0:T(8,128)} %bitcast.3, bf16[256,64]{1,0:T(8,128)(2,1)} %constant.42.clone.refs_2_, bf16[256,64]{1,0:T(8,128)(2,1)} %constant.43.clone.refs_3_, bf16[1024,1024]{1,0:T(8,128)(2,1)} %constant.52.refs_4_, ...), custom_call_target="tpu_custom_call" | custom-call | tf_op jit(solution)/shard_map/pallas_call | solution.py:700
  36.7 0.0 copy-done
  36.7 2.3 %shard_map.182 = f32[16,32,2048]{2,1,0:T(8,128)} custom-call(bf16[448,2048]{1,0:T(8,128)(2,1)S(1)} %shard_map.181.x_ref, bf16[4,128,256]{2,1,0:T(8,128)(2,1)S(1)} %copy-done), custom_call_target="tpu_custom_call" | custom-call | tf_op jit(solution)/shard_map/pallas_call | solution.py:650
Async XLA Ops:
  0.0 36.7 %copy-start = (bf16[4,128,256]{2,1,0:T(8,128)(2,1)S(1)}, bf16[4,128,256]{2,1,0:T(8,128)(2,1)}, u32[]{:S(2)}) copy-start(bf16[4,128,256]{2,1,0:T(8,128)(2,1)} %constant.50.clone.r_ref) | copy-start | bytes 786436

commit v8 on v7

--- a/solution.py
+++ b/solution.py
@@ -461,15 +461,23 @@
     loads = [
         pltpu.make_async_copy(s, t, load_sem.at[i]) for i, (s, t) in enumerate(zip(sources, loaded))
     ]
-    for load in loads[:5]:
+    deep = table_x[0].shape[0] // 2
+    x_halves = [
+        pltpu.make_async_copy(
+            sources[4].at[pl.ds(i * deep, deep)], table_x[0].at[pl.ds(i * deep, deep)],
+            load_sem.at[(4, len(loads))[i]],
+        )
+        for i in range(2)
+    ]
+    for load in loads[:4] + x_halves:
         load.start()
     rows = q_ref.shape[0] // planes
     size = 2 * half
     pitch = sent[0].shape[0] // devices
 
-    def x_lines(chunk, charges):
+    def x_lines(chunk, charges, groups):
         per = LANES // size
-        for group in range(devices // per):
+        for group in groups:
             both = mul(table_x[chunk][group * 2 * LANES : (group + 1) * 2 * LANES, :], charges, ((1,), (1,)))
             made = both[:LANES, :LANES] + both[:LANES, LANES:] + both[LANES:, :LANES]
             step = sent[chunk].shape[0] // devices
@@ -487,19 +495,22 @@
             sent[0][at : at + 8, :] = lines[device * 8 : (device + 1) * 8, :]
     with scope("x_load"):
         loads[0].wait()
-        loads[4].wait()
+        x_halves[0].wait()
+    with scope("x_lines0"):
+        charges = jnp.concatenate(split(q_ref[...]), axis=0)
+        groups = devices * size // LANES
+        x_lines(0, charges, range(groups // 2))
+        x_halves[1].wait()
         for load in loads[5:]:
             load.start()
-    with scope("x_lines0"):
-        charges = jnp.concatenate(split(q_ref[...]), axis=0)
-        x_lines(0, charges)
+        x_lines(0, charges, range(groups // 2, groups))
     with scope("barrier"):
         pl.semaphore_wait(barrier, devices - 1)
     with scope("send0"):
         there = [exchange(blocks_z, blocks_y, size + 2, sent[0], held[0], sent_sem.at[0], 2)]
     with scope("x_lines1"):
         loads[5].wait()
-        x_lines(1, charges)
+        x_lines(1, charges, range(groups))
     with scope("send1"):
         there.append(exchange(blocks_z, blocks_y, size, sent[1], held[1], sent_sem.at[1], 2))
     with scope("wait_there0"):
@@ -704,7 +715,7 @@
         out_specs=pl.BlockSpec(memory_space=pltpu.VMEM),
         scratch_shapes=[
             *(pltpu.VMEM(a.shape, a.dtype) for a in arrays),
-            dma((len(arrays),)), dma((CHUNKS, 2)), dma((CHUNKS, 3)), dma((2, 3)),
+            dma((len(arrays) + 1,)), dma((CHUNKS, 2)), dma((CHUNKS, 3)), dma((2, 3)),
             block(place, 2 * width), block(6 * rows, 2 * width),
             block(devices * (size + 8), LANES), block(deep, LANES),
             block(devices * (size + 8), LANES), block(deep, LANES),

time: 39.1 us -> 39.4 us (level)
  the two profiles are of different devices: /device:TPU:5 before, /device:TPU:16 now
where the time goes in v8:
time: 39.4 us; the launch traced here: 39.2 us
  Pallas kernels  39.2 us (99%)
    pallas_call x1, Pallas kernels, per_device(): pl.pallas_call(functools.partial(main_kernel, (count, blocks_z, blocks_y,...  36.9 us
    pallas_call x1, Pallas kernels, refine(): pl.pallas_call(functools.partial(refine_kernel, rows), out_shape=jax.Shap...  2.31 us

profile of v8, /device:TPU:16, one launch (start us, length us, event | category | flops | bytes accessed | tf_op | source)
XLA Modules:
  0.0 39.2 jit_solution(5054981645043734303)
XLA Ops:
  0.0 0.0 copy-start
  0.0 36.9 %shard_map.181.x_ref = bf16[448,2048]{1,0:T(8,128)(2,1)S(1)} custom-call(f32[128,1024]{1,0:T(8,128)} %bitcast.2, f32[128,64]{1,0:T(8,128)} %bitcast.3, bf16[256,64]{1,0:T(8,128)(2,1)} %constant.42.clone.refs_2_, bf16[256,64]{1,0:T(8,128)(2,1)} %constant.43.clone.refs_3_, bf16[1024,1024]{1,0:T(8,128)(2,1)} %constant.52.refs_4_, ...), custom_call_target="tpu_custom_call" | custom-call | tf_op jit(solution)/shard_map/pallas_call | solution.py:711
  36.9 0.0 copy-done
  36.9 2.3 %shard_map.182 = f32[16,32,2048]{2,1,0:T(8,128)} custom-call(bf16[448,2048]{1,0:T(8,128)(2,1)S(1)} %shard_map.181.x_ref, bf16[4,128,256]{2,1,0:T(8,128)(2,1)S(1)} %copy-done), custom_call_target="tpu_custom_call" | custom-call | tf_op jit(solution)/shard_map/pallas_call | solution.py:661
Async XLA Ops:
  0.0 36.9 %copy-start = (bf16[4,128,256]{2,1,0:T(8,128)(2,1)S(1)}, bf16[4,128,256]{2,1,0:T(8,128)(2,1)}, u32[]{:S(2)}) copy-start(bf16[4,128,256]{2,1,0:T(8,128)(2,1)} %constant.50.clone.r_ref) | copy-start | bytes 786436
